TPU v7x, 32 devices: a 4x2x2 block of a 4x4x8 slice. The times are simulated.
32 devices in a mesh: dp: 4 (over y, z), ep: 8 (over x, core).
Axes of the slice: x: 4, y: 2, z: 2, core: 2. Of those that a mesh axis runs over, the one named last changes fastest.
The devices are a block of a 4x4x8 slice.
Arguments:
- x_rows: bfloat16 [1024, 1536], P(('dp', 'ep')), parts along dimension 0
- expert_idx: int32 [1024, 8], P(('dp', 'ep')), parts along dimension 0
- gate_w: float32 [1024, 8], P(('dp', 'ep')), parts along dimension 0
- slot_pos: int32 [1024, 8], P(('dp', 'ep')), parts along dimension 0
- w_gate: bfloat16 [40, 1536, 512], P('ep')
- w_up: bfloat16 [40, 1536, 512], P('ep')
- w_down: bfloat16 [40, 512, 1536], P('ep')
- grad_out: bfloat16 [1024, 1536], P(('dp', 'ep')), parts along dimension 0
Outputs:
- output 1: bfloat16 [1024, 1536], P(('dp', 'ep')), parts along dimension 0
- output 2: bfloat16 [1024, 1536], P(('dp', 'ep')), parts along dimension 0
- output 3: bfloat16 [160, 1536, 512], P(('dp', 'ep')), parts along dimension 0
- output 4: bfloat16 [160, 1536, 512], P(('dp', 'ep')), parts along dimension 0
- output 5: bfloat16 [160, 512, 1536], P(('dp', 'ep')), parts along dimension 0
- output 6: float32 [1024, 8], P(('dp', 'ep')), parts along dimension 0
There are 4 independent parts. A program takes and returns all parts, laid end to end along the dimension named above; an argument that names none is the same for every part.
All inputs are finite; a program needn't handle non-finite values.
Results may differ from a plain program's by a relative error of at most 0.0103429.
Values are sent between devices in bfloat16 or wider.
A program may use at most 768 MiB of HBM per device.

v0:
```python
import jax
import jax.numpy as jnp
from jax import lax
from jax.sharding import PartitionSpec as P


def capacity_of(tok_dev, top_k, n_experts):
    return ((2 * tok_dev * top_k + n_experts - 1) // n_experts + 7) // 8 * 8


def take_rows(table, where_from):
    return jnp.take(table, where_from, axis=0, mode='fill', fill_value=0)


def solution(mesh):
    group_size = mesh.shape['ep']
    row_spec = P(('dp', 'ep'))
    expert_spec = P('ep')

    def per_device(x_rows, expert_idx, gate_w, slot_pos, w_gate, w_up, w_down, grad_out):
        tok_dev, model_dim = x_rows.shape
        top_k = expert_idx.shape[1]
        local_experts = w_gate.shape[0]
        n_experts = local_experts * group_size
        capacity = capacity_of(tok_dev, top_k, n_experts)
        n_rows = n_experts * capacity
        n_choice = tok_dev * top_k
        buf_shape = (group_size, local_experts, capacity, model_dim)
        flat_pos = jnp.where(slot_pos >= 0, expert_idx * capacity + slot_pos, n_rows).reshape(n_choice)
        src_choice = jnp.full((n_rows,), n_choice, jnp.int32).at[flat_pos].set(jnp.arange(n_choice, dtype=jnp.int32), mode='drop')
        src_tok = src_choice // top_k

        send_x = take_rows(x_rows, src_tok).reshape(buf_shape)
        recv_x = lax.all_to_all(send_x, 'ep', 0, 0, tiled=True)
        pre_gate = jnp.einsum('secd,edf->secf', recv_x, w_gate, preferred_element_type=jnp.float32)
        pre_up = jnp.einsum('secd,edf->secf', recv_x, w_up, preferred_element_type=jnp.float32)
        gate_sig = jax.nn.sigmoid(pre_gate)
        gate_act = pre_gate * gate_sig
        hidden = (gate_act * pre_up).astype(jnp.bfloat16)
        y_rows = jnp.einsum('secf,efd->secd', hidden, w_down, preferred_element_type=jnp.float32).astype(jnp.bfloat16)
        y_back = lax.all_to_all(y_rows, 'ep', 0, 0, tiled=True).reshape(n_rows, model_dim)
        y_choice = take_rows(y_back, flat_pos).reshape(tok_dev, top_k, model_dim)
        out_rows = jnp.sum(gate_w[:, :, None] * y_choice.astype(jnp.float32), axis=1).astype(jnp.bfloat16)
        grad_gate = jnp.einsum('td,tkd->tk', grad_out, y_choice, preferred_element_type=jnp.float32)

        w_rows = take_rows(gate_w.reshape(n_choice), src_choice)
        g_rows = take_rows(grad_out, src_tok)
        send_dy = (w_rows[:, None] * g_rows.astype(jnp.float32)).astype(jnp.bfloat16).reshape(buf_shape)
        recv_dy = lax.all_to_all(send_dy, 'ep', 0, 0, tiled=True)
        d_hidden = jnp.einsum('secd,efd->secf', recv_dy, w_down, preferred_element_type=jnp.float32)
        d_gate = (d_hidden * pre_up * (gate_sig * (1.0 + pre_gate * (1.0 - gate_sig)))).astype(jnp.bfloat16)
        d_up = (d_hidden * gate_act).astype(jnp.bfloat16)
        grad_w_down = jnp.einsum('secf,secd->efd', hidden, recv_dy, preferred_element_type=jnp.float32).astype(jnp.bfloat16)
        grad_w_gate = jnp.einsum('secd,secf->edf', recv_x, d_gate, preferred_element_type=jnp.float32).astype(jnp.bfloat16)
        grad_w_up = jnp.einsum('secd,secf->edf', recv_x, d_up, preferred_element_type=jnp.float32).astype(jnp.bfloat16)
        d_rows = (jnp.einsum('secf,edf->secd', d_gate, w_gate, preferred_element_type=jnp.float32) + jnp.einsum('secf,edf->secd', d_up, w_up, preferred_element_type=jnp.float32)).astype(jnp.bfloat16)
        d_back = lax.all_to_all(d_rows, 'ep', 0, 0, tiled=True).reshape(n_rows, model_dim)
        d_choice = take_rows(d_back, flat_pos).reshape(tok_dev, top_k, model_dim)
        grad_x = jnp.sum(d_choice.astype(jnp.float32), axis=1).astype(jnp.bfloat16)
        return out_rows, grad_x, grad_w_gate, grad_w_up, grad_w_down, grad_gate

    return jax.shard_map(per_device, mesh=mesh,
                         in_specs=(row_spec, row_spec, row_spec, row_spec, expert_spec, expert_spec, expert_spec, row_spec),
                         out_specs=(row_spec, row_spec, row_spec, row_spec, row_spec, row_spec),
                         check_vma=False)
```

profile of v0, /device:TPU:120, one launch (start us, length us, event | category | flops | bytes accessed | tf_op | source)
XLA Modules:
  0.0 152.7 jit_solution(18332038361740095611)
XLA Ops:
  3.9 4.3 %gather_fusion = f32[640]{0:T(1024)S(1)} fusion(f32[256]{0:T(256)S(1)} %reshape.89, s32[1024]{0:T(1024)S(1)} %pad_clamp_fusion), kind=kCustom, calls=%fused_computation.4 | custom fusion | bytes 7680 | tf_op jit(solution)/shard_map/jit(_take)/gather | solution.py:12
  8.2 3.1 %gather_fusion.3 = bf16[640,1536]{1,0:T(8,128)(2,1)S(1)} fusion(bf16[32,1536]{1,0:T(8,128)(2,1)S(1)} %copy-done, s32[1024]{0:T(1024)S(1)} %pad_clamp_fusion.2), kind=kCustom, calls=%fused_computation.2.clone | custom fusion | bytes 3934720 | tf_op jit(solution)/shard_map/jit(_take)/gather | solution.py:12
  11.3 1.8 %multiply_convert_fusion = bf16[640,1536]{1,0:T(8,128)(2,1)} fusion(bf16[640,1536]{1,0:T(8,128)(2,1)S(1)} %gather_fusion.3, f32[640]{0:T(1024)S(1)} %and_select_fusion, pred[640]{0:T(1024)(128)(4,1)S(1)} %get-tuple-element.8), kind=kLoop, calls=%fused_computation.22 | loop fusion | flops 3932160 | bytes 3935360 | tf_op jit(solution)/shard_map/convert_element_type | solution.py:48
  13.1 4.7 %all-to-all-start.2 = ((bf16[8,5,16,1536]{3,2,1,0:T(8,128)(2,1)}), bf16[8,5,16,1536]{3,2,1,0:T(8,128)(2,1)S(1)}, u32[]{:S(2)}, u32[]{:S(2)}) async-start(bf16[8,5,16,1536]{3,2,1,0:T(8,128)(2,1)} %bitcast.80), calls=%async_computation.2 | async-start | bytes 3932160 | tf_op jit(solution)/shard_map/all_to_all | solution.py:49
  17.9 3.7 %gather_fusion.1 = bf16[640,1536]{1,0:T(8,128)(2,1)} fusion(bf16[32,1536]{1,0:T(8,128)(2,1)S(1)} %copy-done.1, s32[1024]{0:T(1024)S(1)} %pad_clamp_fusion.2), kind=kCustom, calls=%fused_computation.clone | custom fusion | bytes 3934720 | tf_op jit(solution)/shard_map/jit(_take)/gather | solution.py:12
  21.5 3.0 %broadcast_select_fusion = bf16[640,1536]{1,0:T(8,128)(2,1)} fusion(bf16[640,1536]{1,0:T(8,128)(2,1)} %gather_fusion.1, pred[640]{0:T(1024)(128)(4,1)S(1)} %get-tuple-element.8), kind=kLoop, calls=%fused_computation.26 | loop fusion | flops 983040 | bytes 3932800 | tf_op jit(solution)/shard_map/jit(_take)/select_n | solution.py:12
  24.6 19.1 %all-to-all-done.2 = bf16[8,5,16,1536]{3,2,1,0:T(8,128)(2,1)S(1)} async-done(((bf16[8,5,16,1536]{3,2,1,0:T(8,128)(2,1)}), bf16[8,5,16,1536]{3,2,1,0:T(8,128)(2,1)S(1)}, u32[]{:S(2)}, u32[]{:S(2)}) %all-to-all-start.2) | async-done | bytes 1966112 | tf_op jit(solution)/shard_map/all_to_all | solution.py:49
  43.6 4.5 %all-to-all-start = ((bf16[8,5,16,1536]{3,2,1,0:T(8,128)(2,1)}), bf16[8,5,16,1536]{3,2,1,0:T(8,128)(2,1)}, u32[]{:S(2)}, u32[]{:S(2)}) async-start(bf16[8,5,16,1536]{3,2,1,0:T(8,128)(2,1)} %bitcast.81), calls=%async_computation | async-start | bytes 3932160 | tf_op jit(solution)/shard_map/all_to_all | solution.py:34
  48.3 5.8 %fusion.27 = f32[8,5,16,512]{3,2,0,1:T(8,128)S(1)} fusion(bf16[5,512,1536]{2,1,0:T(8,128)(2,1)} %param.18, bf16[8,5,16,1536]{3,2,1,0:T(8,128)(2,1)S(1)} %all-to-all-done.2), kind=kOutput, calls=%fused_computation.32 | convolution fusion | flops 1006632960 | bytes 11141120 | tf_op jit(solution)/shard_map/secd,efd->secf/dot_general | solution.py:50
  54.1 19.6 %all-to-all-done = bf16[8,5,16,1536]{3,2,1,0:T(8,128)(2,1)} async-done(((bf16[8,5,16,1536]{3,2,1,0:T(8,128)(2,1)}), bf16[8,5,16,1536]{3,2,1,0:T(8,128)(2,1)}, u32[]{:S(2)}, u32[]{:S(2)}) %all-to-all-start) | async-done | bytes 1966112 | tf_op jit(solution)/shard_map/all_to_all | solution.py:34
  73.7 5.2 %fusion.37 = f32[8,5,16,512]{3,2,0,1:T(8,128)S(1)} fusion(bf16[5,1536,512]{2,1,0:T(8,128)(2,1)} %param.17, bf16[8,5,16,1536]{3,2,1,0:T(8,128)(2,1)} %all-to-all-done), kind=kOutput, calls=%fused_computation.34 | convolution fusion | flops 1006632960 | bytes 11141120 | tf_op jit(solution)/shard_map/secd,edf->secf/dot_general | solution.py:36
  78.9 6.7 %multiply_convert_fusion.2 = (bf16[8,5,16,512]{3,2,0,1:T(8,128)(2,1)}, bf16[8,5,16,512]{3,2,0,1:T(8,128)(2,1)}, bf16[8,5,16,512]{3,2,0,1:T(8,128)(2,1)S(1)}) fusion(f32[8,5,16,512]{3,2,0,1:T(8,128)S(1)} %fusion.27, f32[8,5,16,512]{3,2,0,1:T(8,128)S(1)} %fusion.37, bf16[5,1536,512]{2,1,0:T(8,128)(2,1)} %param.16, bf16[8,5,16,1536]{3,2,1,0:T(8,128)(2,1)} %all-to-all-done), kind=kOutput, calls=%fused_computation.36 | convolution fusion | flops 1011548160 | bytes 14417920 | tf_op jit(solution)/shard_map/secd,edf->secf/dot_general | solution.py:35
  88.2 4.1 %all-to-all-start.1 = ((bf16[8,5,16,1536]{3,2,1,0:T(8,128)(2,1)}), bf16[8,5,16,1536]{3,2,1,0:T(8,128)(2,1)S(1)}, u32[]{:S(2)}, u32[]{:S(2)}) async-start(bf16[8,5,16,1536]{3,2,1,0:T(8,128)(2,1)} %copy.28), calls=%async_computation.1 | async-start | bytes 3932160 | tf_op jit(solution)/shard_map/all_to_all | solution.py:41
  92.4 6.0 %fusion = f32[5,8,16,1536]{3,2,1,0:T(8,128)S(1)} fusion(bf16[8,5,16,512]{3,2,0,1:T(8,128)(2,1)S(1)} %copy-done.4, bf16[5,1536,512]{2,1,0:T(8,128)(2,1)} %param.17), kind=kOutput, calls=%fused_computation.9 | convolution fusion | flops 1006632960 | bytes 12451840 | tf_op jit(solution)/shard_map/secf,edf->secd/dot_general | solution.py:56
  98.5 5.5 %bitcast_convert_fusion = bf16[5,512,1536]{2,1,0:T(8,128)(2,1)} fusion(bf16[8,5,16,512]{3,2,0,1:T(8,128)(2,1)S(1)} %copy-done.7, bf16[8,5,16,1536]{3,2,1,0:T(8,128)(2,1)S(1)} %copy-done.3), kind=kOutput, calls=%fused_computation.6 | convolution fusion | flops 1010565120 | bytes 10485760 | tf_op jit(solution)/shard_map/secf,secd->efd/dot_general | solution.py:53
  104.0 2.7 %fusion.20 = bf16[8,5,16,1536]{3,2,0,1:T(8,128)(2,1)S(1)} fusion(f32[5,8,16,1536]{3,2,1,0:T(8,128)S(1)} %fusion, bf16[8,5,16,512]{3,2,0,1:T(8,128)(2,1)S(1)} %copy-done.5, bf16[5,1536,512]{2,1,0:T(8,128)(2,1)S(1)} %bitcast.79), kind=kOutput, calls=%fused_computation.25 | convolution fusion | flops 1008599040 | bytes 14417920 | tf_op jit(solution)/shard_map/secf,edf->secd/dot_general | solution.py:56
  106.6 1.4 copy.31
  108.1 7.0 %bitcast_convert_fusion.2 = bf16[5,1536,512]{2,1,0:T(8,128)(2,1)} fusion(bf16[8,5,16,1536]{3,2,1,0:T(8,128)(2,1)} %all-to-all-done, bf16[8,5,16,512]{3,2,0,1:T(8,128)(2,1)S(1)} %copy-done.5), kind=kOutput, calls=%fused_computation.8 | convolution fusion | flops 1010565120 | bytes 10485760 | tf_op jit(solution)/shard_map/secd,secf->edf/dot_general | solution.py:54
  115.1 2.6 %all-to-all-done.1 = bf16[8,5,16,1536]{3,2,1,0:T(8,128)(2,1)S(1)} async-done(((bf16[8,5,16,1536]{3,2,1,0:T(8,128)(2,1)}), bf16[8,5,16,1536]{3,2,1,0:T(8,128)(2,1)S(1)}, u32[]{:S(2)}, u32[]{:S(2)}) %all-to-all-start.1) | async-done | bytes 1966112 | tf_op jit(solution)/shard_map/all_to_all | solution.py:41
  117.7 4.7 %all-to-all-start.3 = ((bf16[8,5,16,1536]{3,2,1,0:T(8,128)(2,1)}), bf16[8,5,16,1536]{3,2,1,0:T(8,128)(2,1)}, u32[]{:S(2)}, u32[]{:S(2)}) async-start(bf16[8,5,16,1536]{3,2,1,0:T(8,128)(2,1)} %copy.31), calls=%async_computation.3 | async-start | bytes 3932160 | tf_op jit(solution)/shard_map/all_to_all | solution.py:57
  122.5 7.0 %bitcast_convert_fusion.1 = bf16[5,1536,512]{2,1,0:T(8,128)(2,1)} fusion(bf16[8,5,16,1536]{3,2,1,0:T(8,128)(2,1)} %all-to-all-done, bf16[8,5,16,512]{3,2,0,1:T(8,128)(2,1)S(1)} %copy-done.4), kind=kOutput, calls=%fused_computation.7 | convolution fusion | flops 1010565120 | bytes 10485760 | tf_op jit(solution)/shard_map/secd,secf->edf/dot_general | solution.py:55
  132.2 1.5 multiply_reduce_fusion
  133.6 14.2 %all-to-all-done.3 = bf16[8,5,16,1536]{3,2,1,0:T(8,128)(2,1)} async-done(((bf16[8,5,16,1536]{3,2,1,0:T(8,128)(2,1)}), bf16[8,5,16,1536]{3,2,1,0:T(8,128)(2,1)}, u32[]{:S(2)}, u32[]{:S(2)}) %all-to-all-start.3) | async-done | bytes 1966112 | tf_op jit(solution)/shard_map/all_to_all | solution.py:57
  147.8 3.8 %gather_fusion.4 = bf16[256,1536]{1,0:T(8,128)(2,1)S(1)} fusion(bf16[640,1536]{1,0:T(8,128)(2,1)} %bitcast.19, s32[1024]{0:T(1024)S(1)} %pad_clamp_fusion.1), kind=kCustom, calls=%fused_computation.3.clone | custom fusion | bytes 1573888 | tf_op jit(solution)/shard_map/jit(_take)/gather | solution.py:12
  (49 shorter events, 9.7 us)
Async XLA Ops:
  0.6 7.6 %copy-start = (bf16[32,1536]{1,0:T(8,128)(2,1)S(1)}, bf16[32,1536]{1,0:T(8,128)(2,1)}, u32[]{:S(2)}) copy-start(bf16[32,1536]{1,0:T(8,128)(2,1)} %param.19) | copy-start | bytes 294916
  13.1 4.7 %copy-start.1 = (bf16[32,1536]{1,0:T(8,128)(2,1)S(1)}, bf16[32,1536]{1,0:T(8,128)(2,1)}, u32[]{:S(2)}) copy-start(bf16[32,1536]{1,0:T(8,128)(2,1)} %param.12) | copy-start | bytes 294916
  13.1 30.5 %all-to-all-start.2 = ((bf16[8,5,16,1536]{3,2,1,0:T(8,128)(2,1)}), bf16[8,5,16,1536]{3,2,1,0:T(8,128)(2,1)S(1)}, u32[]{:S(2)}, u32[]{:S(2)}) async-start(bf16[8,5,16,1536]{3,2,1,0:T(8,128)(2,1)} %bitcast.80), calls=%async_computation.2 | async-start | bytes 3932160 | tf_op jit(solution)/shard_map/all_to_all | solution.py:49
  43.6 4.6 %copy-start.2 = (bf16[8,5,16,1536]{3,2,1,0:T(8,128)(2,1)}, bf16[8,5,16,1536]{3,2,1,0:T(8,128)(2,1)S(1)}, u32[]{:S(2)}) copy-start(bf16[8,5,16,1536]{3,2,1,0:T(8,128)(2,1)S(1)} %all-to-all-done.2) | copy-start | bytes 5898244
  43.6 30.1 %all-to-all-start = ((bf16[8,5,16,1536]{3,2,1,0:T(8,128)(2,1)}), bf16[8,5,16,1536]{3,2,1,0:T(8,128)(2,1)}, u32[]{:S(2)}, u32[]{:S(2)}) async-start(bf16[8,5,16,1536]{3,2,1,0:T(8,128)(2,1)} %bitcast.81), calls=%async_computation | async-start | bytes 3932160 | tf_op jit(solution)/shard_map/all_to_all | solution.py:34
  73.7 11.9 %slice-start = ((s8[7864320]{0:T(1024)(128)(4,1)}), s8[4194304]{0:T(1024)(128)(4,1)S(1)}, s32[]{:S(2)}) async-start(s8[7864320]{0:T(1024)(128)(4,1)} %bitcast.75), calls=%async_computation.4 | async-start | bytes 8388608
  78.9 6.7 %slice-start.1 = ((s8[7864320]{0:T(1024)(128)(4,1)}), s8[3670016]{0:T(1024)(128)(4,1)S(1)}, s32[]{:S(2)}) async-start(s8[7864320]{0:T(1024)(128)(4,1)} %bitcast.75), calls=%async_computation.5 | async-start | bytes 7340032
  85.6 1.2 copy-start.6
  88.2 4.1 %copy-start.4 = (bf16[8,5,16,512]{3,2,0,1:T(8,128)(2,1)S(1)}, bf16[8,5,16,512]{3,2,0,1:T(8,128)(2,1)}, u32[]{:S(2)}) copy-start(bf16[8,5,16,512]{3,2,0,1:T(8,128)(2,1)} %get-tuple-element.11) | copy-start | bytes 1966084
  88.2 29.5 %all-to-all-start.1 = ((bf16[8,5,16,1536]{3,2,1,0:T(8,128)(2,1)}), bf16[8,5,16,1536]{3,2,1,0:T(8,128)(2,1)S(1)}, u32[]{:S(2)}, u32[]{:S(2)}) async-start(bf16[8,5,16,1536]{3,2,1,0:T(8,128)(2,1)} %copy.28), calls=%async_computation.1 | async-start | bytes 3932160 | tf_op jit(solution)/shard_map/all_to_all | solution.py:41
  92.4 6.1 %copy-start.3 = (bf16[8,5,16,1536]{3,2,1,0:T(8,128)(2,1)S(1)}, bf16[8,5,16,1536]{3,2,1,0:T(8,128)(2,1)}, u32[]{:S(2)}) copy-start(bf16[8,5,16,1536]{3,2,1,0:T(8,128)(2,1)} %copy-done.2) | copy-start | bytes 5898244
  92.4 6.1 %copy-start.7 = (bf16[8,5,16,512]{3,2,0,1:T(8,128)(2,1)S(1)}, bf16[8,5,16,512]{3,2,0,1:T(8,128)(2,1)}, u32[]{:S(2)}) copy-start(bf16[8,5,16,512]{3,2,0,1:T(8,128)(2,1)} %copy-done.6) | copy-start | bytes 1966084
  92.4 11.6 %slice-start.2 = ((s8[7864320]{0:T(1024)(128)(4,1)}), s8[4194304]{0:T(1024)(128)(4,1)S(1)}, s32[]{:S(2)}) async-start(s8[7864320]{0:T(1024)(128)(4,1)} %bitcast.78), calls=%async_computation.6 | async-start | bytes 8388608
  98.4 5.5 %slice-start.3 = ((s8[7864320]{0:T(1024)(128)(4,1)}), s8[3670016]{0:T(1024)(128)(4,1)S(1)}, s32[]{:S(2)}) async-start(s8[7864320]{0:T(1024)(128)(4,1)} %bitcast.78), calls=%async_computation.7 | async-start | bytes 7340032
  98.5 5.5 %copy-start.5 = (bf16[8,5,16,512]{3,2,0,1:T(8,128)(2,1)S(1)}, bf16[8,5,16,512]{3,2,0,1:T(8,128)(2,1)}, u32[]{:S(2)}) copy-start(bf16[8,5,16,512]{3,2,0,1:T(8,128)(2,1)} %get-tuple-element.10) | copy-start | bytes 1966084
  117.7 30.1 %all-to-all-start.3 = ((bf16[8,5,16,1536]{3,2,1,0:T(8,128)(2,1)}), bf16[8,5,16,1536]{3,2,1,0:T(8,128)(2,1)}, u32[]{:S(2)}, u32[]{:S(2)}) async-start(bf16[8,5,16,1536]{3,2,1,0:T(8,128)(2,1)} %copy.31), calls=%async_computation.3 | async-start | bytes 3932160 | tf_op jit(solution)/shard_map/all_to_all | solution.py:57
where the time goes:
time: 154 us; the launch traced here: 153 us
  waiting for transfers between devices  55.5 us (36%)
  matrix products  47.8 us (31%)
  local copies, waits for them, and re-layouts  22.2 us (14%)
  starting transfers between devices  18.1 us (12%)
  other arithmetic  8.18 us (5%)
    all_to_all x1, waiting for transfers between devices, per_device(): recv_x = lax.all_to_all(send_x, 'ep', 0, 0, tiled=True)  19.6 us
    all_to_all x1, waiting for transfers between devices, per_device(): recv_dy = lax.all_to_all(send_dy, 'ep', 0, 0, tiled=True)  19.1 us
    gather x5, local copies, waits for them, and re-layouts, take_rows(): return jnp.take(table, where_from, axis=0, mode='fill', fill_value=0)  16.1 us
    all_to_all x1, waiting for transfers between devices, per_device(): lax.all_to_all(d_rows, 'ep', 0, 0, tiled=True).reshape(n_rows, model_dim)  14.2 us
    dot_general x1, matrix products, per_device(): jnp.einsum('secd,secf->edf', recv_x, d_gate, preferred_element_type=jnp.f...  7.02 us
    dot_general x1, matrix products, per_device(): jnp.einsum('secd,secf->edf', recv_x, d_up, preferred_element_type=jnp.flo...  7.02 us
    dot_general x1, matrix products, per_device(): jnp.einsum('secd,edf->secf', recv_x, w_gate, preferred_element_type=jnp.f...  6.69 us
    dot_general x1, matrix products, per_device(): jnp.einsum('secf,edf->secd', d_up, w_up, preferred_element_type=jnp.float32)  6.02 us
  transfers between devices with their start and end apart: 4, of which 4 were waited for; matrix products, arithmetic and copies ran while one was open for 30% of the time, Pallas kernels for 0%

commit v1 on v0

v1 whole, which is shorter than its diff:
```python
import functools

import jax
import jax.numpy as jnp
from jax import lax
from jax.experimental import pallas as pl
from jax.experimental.pallas import tpu as pltpu
from jax.sharding import PartitionSpec as P

BF16, F32 = jnp.bfloat16, jnp.float32
MESH_ID = pl.DeviceIdType.MESH
ANY = pl.ANY
LANES = 128


def capacity_of(tok_dev, top_k, n_experts):
    return ((2 * tok_dev * top_k + n_experts - 1) // n_experts + 7) // 8 * 8


def dot_nn(a, b):
    return lax.dot_general(a, b, (((1,), (0,)), ((), ())), preferred_element_type=F32)


def dot_nt(a, b):
    return lax.dot_general(a, b, (((1,), (1,)), ((), ())), preferred_element_type=F32)


def dot_tn(a, b):
    return lax.dot_general(a, b, (((0,), (0,)), ((), ())), preferred_element_type=F32)


def moe_kernel(dims, x_hbm, g_hbm, idx_ref, slot_ref, gate_ref, w1_hbm, w3_hbm, w2_hbm,
               out_ref, gx_ref, gg_ref, r_hbm, dy_hbm, h_hbm, da_hbm, db_hbm,
               w1, w3, w2, xg, meta, scr, scr2, r_all, dy_all, h_all, da_all, db_all, c1_all, c2_all,
               p_all, gs_all, y_all, dr_all, part, sibbuf, ringbuf, finbuf, ggsrc, ggbuf,
               w_sem, loc_sem, wb_sem, meta_ss, meta_rs, ag_ss, ag_rs, rt_ss, rt_rs, gg_ss, gg_rs):
    G, T, D, F, E, C, K = dims
    NQ = G // 2
    RW = G * C
    DH = D // 2
    per_tile = LANES // T
    me = lax.axis_index("ep")
    core = lax.rem(me, 2)
    chip = me // 2
    right_chip, left_chip, opp_chip = (lax.rem(chip + 1, NQ), lax.rem(chip + NQ - 1, NQ), lax.rem(chip + 2, NQ))
    dev = lambda q, c: q * 2 + c
    other = 1 - core
    sib = dev(chip, other)
    right, left, opp = dev(right_chip, core), dev(left_chip, core), dev(opp_chip, core)

    w_copies = []
    for e in range(E):
        for k, (src, dst) in enumerate(((w1_hbm, w1), (w3_hbm, w3), (w2_hbm, w2))):
            w_copies.append(pltpu.make_async_copy(src.at[e], dst.at[e], w_sem.at[k, e]))

    def rows(d):
        return pl.ds(pl.multiple_of(d * T, T), T)

    own_x = pltpu.make_async_copy(x_hbm, xg.at[0, rows(me)], loc_sem.at[0])
    own_g = pltpu.make_async_copy(g_hbm, xg.at[1, rows(me)], loc_sem.at[1])
    own_x.start()
    own_g.start()
    for cp in w_copies:
        cp.start()

    off = pl.multiple_of(lax.rem(me, per_tile) * T, T)
    scr[...] = jnp.zeros_like(scr)
    scr2[...] = jnp.zeros_like(scr2)
    code = jnp.where(slot_ref[...] >= 0, idx_ref[...] * C + slot_ref[...] + 1, 0)
    scr[pl.ds(off, T), 0:K] = code.astype(F32)
    scr2[pl.ds(off, T), 0:K] = gate_ref[...]
    meta[me, 0:K] = jnp.transpose(scr[...])[0:K]
    meta[me, K:2 * K] = jnp.transpose(scr2[...])[0:K]

    barrier = pltpu.get_barrier_semaphore()
    for d in range(1, G):
        pl.semaphore_signal(barrier, inc=1, device_id={"ep": lax.rem(me + d, G)}, device_id_type=MESH_ID)
    pl.semaphore_wait(barrier, G - 1)

    def remote(src, dst, ss, rs, target):
        return pltpu.make_async_remote_copy(src_ref=src, dst_ref=dst, send_sem=ss, recv_sem=rs,
                                            device_id={"ep": target}, device_id_type=MESH_ID)

    meta_sends = []
    for d in range(1, G):
        cp = remote(meta.at[me], meta.at[me], meta_ss.at[d - 1], meta_rs.at[d - 1], lax.rem(me + d, G))
        cp.start()
        meta_sends.append(cp)

    lo, hi, full = pl.ds(0, DH), pl.ds(DH, DH), pl.ds(0, D)

    def ag(t, k, src_dev, cols, target):
        ref = xg.at[t, rows(src_dev), cols]
        return remote(ref, ref, ag_ss.at[t, k], ag_rs.at[t, k], target)

    sib_right, sib_left, sib_opp = dev(right_chip, other), dev(left_chip, other), dev(opp_chip, other)
    send_desc = lambda t: [ag(t, 0, me, full, sib), ag(t, 1, me, lo, right), ag(t, 2, me, hi, right),
                           ag(t, 3, me, hi, left), ag(t, 4, me, lo, left),
                           ag(t, 5, left, lo, right), ag(t, 6, right, hi, left),
                           ag(t, 7, left, full, sib), ag(t, 8, right, full, sib),
                           ag(t, 9, opp, lo, sib), ag(t, 10, opp, hi, sib)]
    recv_desc = lambda t: [ag(t, 0, sib, full, sib), ag(t, 1, left, lo, left), ag(t, 2, left, hi, left),
                           ag(t, 3, right, hi, right), ag(t, 4, right, lo, right),
                           ag(t, 5, opp, lo, left), ag(t, 6, opp, hi, right),
                           ag(t, 7, sib_left, full, sib), ag(t, 8, sib_right, full, sib),
                           ag(t, 9, sib_opp, lo, sib), ag(t, 10, sib_opp, hi, sib)]
    sx, sg = send_desc(0), send_desc(1)
    rx, rg = recv_desc(0), recv_desc(1)

    own_x.wait()
    for k in (1, 3, 2, 4, 0):
        sx[k].start()
    own_g.wait()
    rx[1].wait_recv()
    sx[5].start()
    rx[3].wait_recv()
    sx[6].start()
    for k in (1, 3, 2, 4, 0):
        sg[k].start()
    rx[2].wait_recv()
    sx[7].start()
    rx[4].wait_recv()
    sx[8].start()
    rx[5].wait_recv()
    sx[9].start()
    rx[6].wait_recv()
    sx[10].start()
    for d in range(1, G):
        src = lax.rem(me + G - d, G)
        remote(meta.at[src], meta.at[src], meta_ss.at[d - 1], meta_rs.at[d - 1], src).wait_recv()
    for k in (0, 7, 8, 9, 10):
        rx[k].wait_recv()
    rg[1].wait_recv()
    sg[5].start()
    rg[3].wait_recv()
    sg[6].start()

    n_tiles = G // per_tile
    halves = []
    for i in range(n_tiles):
        tot = meta[i * per_tile]
        for s in range(i * per_tile + 1, (i + 1) * per_tile):
            tot = tot + meta[s]
        halves.append(tot)
    codes = jnp.concatenate([v[0:K] for v in halves], axis=1)
    gates = jnp.concatenate([v[K:2 * K] for v in halves], axis=1)
    NT = G * T
    lane_src = (lax.broadcasted_iota(jnp.int32, (K, NT), 1) // T * C).astype(F32)
    row_id = lax.broadcasted_iota(jnp.int32, (RW, NT), 0).astype(F32) + 1.0

    def routing(e):
        first = ((me * E + e) * C).astype(F32) + 1.0
        sel = (codes >= first) & (codes < first + float(C))
        pos = jnp.sum(jnp.where(sel, codes - first + lane_src + 1.0, 0.0), axis=0, keepdims=True)
        return sel, row_id == pos

    def erow(e):
        return pl.ds(pl.multiple_of(e * RW, RW), RW)

    def fwd(e, carry):
        sel, mask = routing(e)
        gate_row = jnp.sum(jnp.where(sel, gates, 0.0), axis=0, keepdims=True)
        p_e = jnp.where(mask, 1.0, 0.0).astype(BF16)
        p_all[erow(e), :] = p_e
        rest = gate_row
        for part_i in range(3):
            piece = rest.astype(BF16).astype(F32)
            gs_all[part_i, erow(e), :] = jnp.where(mask, piece, 0.0).astype(BF16)
            rest = rest - piece
        r_e = dot_nn(p_e, xg[0]).astype(BF16)
        r_all[e] = r_e
        for k in range(3):
            pltpu.make_async_copy((w1_hbm, w3_hbm, w2_hbm)[k].at[e], (w1, w3, w2)[k].at[e], w_sem.at[k, e]).wait()
        a = dot_nn(r_e, w1[e])
        b = dot_nn(r_e, w3[e])
        s = jax.nn.sigmoid(a)
        act = a * s
        h_e = (act * b).astype(BF16)
        h_all[e] = h_e
        c1_all[e] = b * (s * (1.0 + a * (1.0 - s)))
        c2_all[e] = act
        y_all[erow(e), :] = dot_nn(h_e, w2[e]).astype(BF16)

        @pl.when(e == 1)
        def _():
            rg[2].wait_recv()
            sg[7].start()
            rg[4].wait_recv()
            sg[8].start()

        @pl.when(e == 2)
        def _():
            rg[5].wait_recv()
            sg[9].start()
            rg[6].wait_recv()
            sg[10].start()

        return carry

    lax.fori_loop(0, E, fwd, 0)

    def back(t, n, src, dst, target):
        return remote(src, dst, rt_ss.at[t, n], rt_rs.at[t, n], target)

    chips = (opp_chip, right_chip, left_chip, chip)

    def ret_sib_send(t):
        return [back(t, i, part.at[t, rows(dev(q, other))], sibbuf.at[t, i], sib) for i, q in enumerate(chips)]

    def ret_ring_send(t):
        return [back(t, 4, part.at[t, rows(opp), lo], ringbuf.at[t, 0], right),
                back(t, 5, part.at[t, rows(opp), hi], ringbuf.at[t, 1], left),
                back(t, 6, part.at[t, rows(right), hi], finbuf.at[t, 0, :, hi], right),
                back(t, 7, part.at[t, rows(left), lo], finbuf.at[t, 1, :, lo], left),
                back(t, 8, part.at[t, rows(right), lo], finbuf.at[t, 0, :, lo], right),
                back(t, 9, part.at[t, rows(left), hi], finbuf.at[t, 1, :, hi], left)]

    def ret_1(t):
        sends, ring = ret_sib_send(t), ret_ring_send(t)
        for i, d in enumerate((opp, right, left)):
            sends[i].wait_recv()
            part[t, rows(d), :] += sibbuf[t, i]
            if i == 0:
                ring[0].start()
                ring[1].start()
            if i == 1:
                ring[2].start()
            if i == 2:
                ring[3].start()
        sends[3].wait_recv()
        part[t, rows(me), :] += sibbuf[t, 3]

    def ret_2(t):
        ring = ret_ring_send(t)
        ring[0].wait_recv()
        part[t, rows(right), lo] += ringbuf[t, 0]
        ring[4].start()
        ring[1].wait_recv()
        part[t, rows(left), hi] += ringbuf[t, 1]
        ring[5].start()

    def ret_3(t, res_ref):
        ring = ret_ring_send(t)
        for n in (2, 3, 4, 5):
            ring[n].wait_recv()
        res_ref[...] = (part[t, rows(me), :] + finbuf[t, 0] + finbuf[t, 1]).astype(BF16)
        for cp in ret_sib_send(t) + ring:
            cp.wait_send()

    acc = dot_tn(gs_all[0], y_all[...])
    for i in (1, 2):
        acc = acc + dot_tn(gs_all[i], y_all[...])
    part[0] = acc
    for cp in ret_sib_send(0):
        cp.start()

    for k in (0, 7, 8, 9, 10):
        rg[k].wait_recv()

    def bwd(e, gg):
        sel, mask = routing(e)
        gate_row = jnp.sum(jnp.where(sel, gates, 0.0), axis=0, keepdims=True)
        gate_col = jnp.sum(jnp.where(mask, gate_row, 0.0), axis=1, keepdims=True)
        g_e = dot_nn(p_all[erow(e), :], xg[1])
        gg_col = jnp.sum(g_e * y_all[erow(e), :].astype(F32), axis=1, keepdims=True)
        gg_row = jnp.sum(jnp.where(mask, gg_col, 0.0), axis=0, keepdims=True)
        gg = gg + jnp.where(sel, gg_row, 0.0)
        dy_e = (gate_col * g_e).astype(BF16)
        dy_all[e] = dy_e
        dh = dot_nt(dy_e, w2[e])
        da_e = (dh * c1_all[e]).astype(BF16)
        db_e = (dh * c2_all[e]).astype(BF16)
        da_all[e] = da_e
        db_all[e] = db_e
        dr_all[erow(e), :] = (dot_nt(da_e, w1[e]) + dot_nt(db_e, w3[e])).astype(BF16)

        @pl.when(e == 1)
        def _():
            ret_1(0)

        @pl.when(e == 3)
        def _():
            ret_2(0)

        return gg

    gg = lax.fori_loop(0, E, bwd, jnp.zeros((K, NT), F32))
    for i in range(n_tiles):
        ggsrc[i] = gg[:, i * LANES:(i + 1) * LANES]
    part[1] = dot_tn(p_all[...], dr_all[...])
    for cp in ret_sib_send(1):
        cp.start()
    gg_sends = []
    for d in range(1, G):
        tgt = lax.rem(me + d, G)
        cp = remote(ggsrc.at[tgt // per_tile], ggbuf.at[d - 1], gg_ss.at[d - 1], gg_rs.at[d - 1], tgt)
        cp.start()
        gg_sends.append(cp)
    wb = [pltpu.make_async_copy(src, dst, wb_sem.at[i]) for i, (src, dst) in enumerate(
        ((r_all, r_hbm), (dy_all, dy_hbm), (h_all, h_hbm), (da_all, da_hbm), (db_all, db_hbm)))]
    for cp in wb:
        cp.start()
    ret_3(0, out_ref)
    ret_1(1)
    tot = ggsrc[me // per_tile]
    for d in range(1, G):
        gg_sends[d - 1].wait_recv()
        tot = tot + ggbuf[d - 1]
    scr[0:K, :] = tot
    scr2[...] = jnp.transpose(scr[...])
    gg_ref[...] = scr2[pl.ds(off, T), 0:K]
    ret_2(1)
    for cp in meta_sends + sx + sg + gg_sends:
        cp.wait_send()
    for cp in wb:
        cp.wait()
    ret_3(1, gx_ref)


def wgrad_kernel(r_ref, dy_ref, h_ref, da_ref, db_ref, o_in, gx_in, gg_in,
                 g1_ref, g3_ref, g2_ref, o_ref, gx_ref, gg_ref):
    r = r_ref[...]
    g1_ref[...] = dot_tn(r, da_ref[...]).astype(BF16)
    g3_ref[...] = dot_tn(r, db_ref[...]).astype(BF16)
    g2_ref[...] = dot_tn(h_ref[...], dy_ref[...]).astype(BF16)

    @pl.when(pl.program_id(0) == 0)
    def _():
        o_ref[...] = o_in[...]
        gx_ref[...] = gx_in[...]
        gg_ref[...] = gg_in[...]


def solution(mesh):
    group_size = mesh.shape['ep']
    row_spec = P(('dp', 'ep'))
    expert_spec = P('ep')

    def per_device(x_rows, expert_idx, gate_w, slot_pos, w_gate, w_up, w_down, grad_out):
        T, D = x_rows.shape
        K = expert_idx.shape[1]
        E, _, F = w_gate.shape
        G = group_size
        C = capacity_of(T, K, E * G)
        RW, NT = G * C, G * T
        NQ = G // 2
        dims = (G, T, D, F, E, C, K)
        sds = jax.ShapeDtypeStruct
        vm = pltpu.VMEM
        dma = pltpu.SemaphoreType.DMA
        vspec = pl.BlockSpec(memory_space=pltpu.VMEM)
        aspec = pl.BlockSpec(memory_space=ANY)
        out, gx, gg, r, dy, h, da, db = pl.pallas_call(
            functools.partial(moe_kernel, dims),
            out_shape=(sds((T, D), BF16), sds((T, D), BF16), sds((T, K), F32),
                       sds((E, RW, D), BF16), sds((E, RW, D), BF16),
                       sds((E, RW, F), BF16), sds((E, RW, F), BF16), sds((E, RW, F), BF16)),
            in_specs=[aspec, aspec, vspec, vspec, vspec, aspec, aspec, aspec],
            out_specs=(vspec, vspec, vspec, aspec, aspec, aspec, aspec, aspec),
            scratch_shapes=[
                vm((E, D, F), BF16), vm((E, D, F), BF16), vm((E, F, D), BF16),
                vm((2, NT, D), BF16), vm((G, 2 * K, LANES), F32),
                vm((LANES, LANES), F32), vm((LANES, LANES), F32),
                vm((E, RW, D), BF16), vm((E, RW, D), BF16),
                vm((E, RW, F), BF16), vm((E, RW, F), BF16), vm((E, RW, F), BF16),
                vm((E, RW, F), F32), vm((E, RW, F), F32),
                vm((E * RW, NT), BF16), vm((3, E * RW, NT), BF16),
                vm((E * RW, D), BF16), vm((E * RW, D), BF16),
                vm((2, NT, D), F32), vm((2, NQ, T, D), F32),
                vm((2, 2, T, D // 2), F32), vm((2, 2, T, D), F32),
                vm((NT // LANES, K, LANES), F32), vm((G - 1, K, LANES), F32),
                dma((3, E)), dma((2,)), dma((5,)), dma((G - 1,)), dma((G - 1,)),
                dma((2, 11)), dma((2, 11)), dma((2, 10)), dma((2, 10)), dma((G - 1,)), dma((G - 1,)),
            ],
            compiler_params=pltpu.CompilerParams(
                collective_id=0, has_side_effects=True, vmem_limit_bytes=60 * 2 ** 20),
            name="moe_exchange",
        )(x_rows, grad_out, expert_idx, slot_pos, gate_w, w_gate, w_up, w_down)

        blk = lambda *s: pl.BlockSpec((pl.Squeezed(),) + s, lambda e: (e,) + (0,) * len(s))
        whole = lambda *s: pl.BlockSpec(s, lambda e: (0,) * len(s))
        g1, g3, g2, out, gx, gg = pl.pallas_call(
            wgrad_kernel,
            grid=(E,),
            out_shape=(sds((E, D, F), BF16), sds((E, D, F), BF16), sds((E, F, D), BF16),
                       sds((T, D), BF16), sds((T, D), BF16), sds((T, K), F32)),
            in_specs=[blk(RW, D), blk(RW, D), blk(RW, F), blk(RW, F), blk(RW, F),
                      whole(T, D), whole(T, D), whole(T, K)],
            out_specs=(blk(D, F), blk(D, F), blk(F, D), whole(T, D), whole(T, D), whole(T, K)),
            compiler_params=pltpu.CompilerParams(vmem_limit_bytes=40 * 2 ** 20),
            name="weight_grads",
        )(r, dy, h, da, db, out, gx, gg)
        return out, gx, g1, g3, g2, gg

    return jax.shard_map(per_device, mesh=mesh,
                         in_specs=(row_spec, row_spec, row_spec, row_spec, expert_spec, expert_spec, expert_spec, row_spec),
                         out_specs=(row_spec, row_spec, row_spec, row_spec, row_spec, row_spec),
                         check_vma=False)
```

time: 154 us -> 75 us (0.49)
  Pallas kernels: 0 us -> 60.1 us
  waiting for transfers between devices: 55.5 us -> 0 us
  matrix products: 47.8 us -> 0 us
  starting transfers between devices: 18.1 us -> 0 us
  local copies, waits for them, and re-layouts: 22.2 us -> 13.6 us
  other arithmetic: 8.18 us -> 0 us
    pallas_call x0 -> x2, Pallas kernels: none -> 60.1 us  [the longest x1 49.5 us: per_device(): pl.pallas_call(functools.partial(moe_kernel, dims), out_shape=(sds((T, D)...]
    all_to_all x4 -> x0, waiting for transfers between devices: 55.5 us -> none  [the longest x1 19.6 us: per_device(): recv_x = lax.all_to_all(send_x, 'ep', 0, 0, tiled=True)]
    dot_general x10 -> x0, matrix products: 47.8 us -> none  [the longest x1 7.02 us: per_device(): jnp.einsum('secd,secf->edf', recv_x, d_gate, preferred_element_type=jnp.f...]
    all_to_all x4 -> x0, starting transfers between devices: 18.1 us -> none  [the longest x1 4.74 us: per_device(): lax.all_to_all(d_rows, 'ep', 0, 0, tiled=True).reshape(n_rows, model_dim)]
    gather x5 -> x0, local copies, waits for them, and re-layouts: 16.1 us -> none  [take_rows(): return jnp.take(table, where_from, axis=0, mode='fill', fill_value=0)]
    unnamed x25 -> x20, local copies, waits for them, and re-layouts: 0.83 us -> 13.6 us
    select_n x6 -> x0, other arithmetic: 3.79 us -> none  [the longest x4 3.04 us: take_rows(): return jnp.take(table, where_from, axis=0, mode='fill', fill_value=0)]
    convert_element_type x2 -> x0, local copies, waits for them, and re-layouts: 2.83 us -> none  [the longest x1 1.43 us: per_device(): (jnp.einsum('secf,edf->secd', d_gate, w_gate, preferred_element_type=jnp....]
  transfers between devices with their start and end apart: 4 -> 0, of which waited for: 4 -> 0; matrix products, arithmetic and copies ran while one was open for 30% -> 0% of each run, Pallas kernels for 0% -> 0%
where the time goes in v1:
time: 75 us; the launch traced here: 74.4 us
  Pallas kernels  60.1 us (80%)
  local copies, waits for them, and re-layouts  13.6 us (18%)
    pallas_call x1, Pallas kernels, per_device(): pl.pallas_call(functools.partial(moe_kernel, dims), out_shape=(sds((T, D)...  49.5 us
    unnamed x20, local copies, waits for them, and re-layouts  13.6 us
    pallas_call x1, Pallas kernels, per_device(): pl.pallas_call(wgrad_kernel, grid=(E,), out_shape=(sds((E, D, F), BF16),...  10.6 us

profile of v1, /device:TPU:120, one launch (start us, length us, event | category | flops | bytes accessed | tf_op | source)
XLA Modules:
  0.0 74.4 jit_solution(16229347202884037550)
XLA Ops:
  0.6 1.4 %copy.14.idx_ref = s32[32,8]{1,0:T(8,128)} copy(s32[32,8]{0,1:T(8,128)} %param.9) | data formatting | bytes 2048 | tf_op args[1]
  2.0 1.4 %copy.16.gate_ref = f32[32,8]{1,0:T(8,128)} copy(f32[32,8]{0,1:T(8,128)} %param.10) | data formatting | bytes 2048 | tf_op args[2]
  3.4 1.4 %copy.15.slot_ref = s32[32,8]{1,0:T(8,128)} copy(s32[32,8]{0,1:T(8,128)} %param.11) | data formatting | bytes 2048 | tf_op args[3]
  4.7 49.5 %moe_exchange.1 = (bf16[32,1536]{1,0:T(8,128)(2,1)}, bf16[32,1536]{1,0:T(8,128)(2,1)}, f32[32,8]{1,0:T(8,128)}, bf16[5,128,1536]{2,1,0:T(8,128)(2,1)}, bf16[5,12...) custom-call(bf16[32,1536]{1,0:T(8,128)(2,1)} %x_hbm.1, ...), custom_call_target="tpu_custom_call" | custom-call | tf_op jit(solution)/shard_map/moe_exchange/pallas_call | solution.py:353
  54.2 0.0 copy-start
  54.2 1.5 %copy-done = bf16[5,128,1536]{2,1,0:T(8,128)(2,1)S(1)} copy-done((bf16[5,128,1536]{2,1,0:T(8,128)(2,1)S(1)}, bf16[5,128,1536]{2,1,0:T(8,128)(2,1)}, u32[]{:S(2)}) %copy-start) | copy-done | bytes 1966104
  55.8 0.0 copy-start.1
  55.8 1.5 %copy-done.1 = bf16[5,128,1536]{2,1,0:T(8,128)(2,1)S(1)} copy-done((bf16[5,128,1536]{2,1,0:T(8,128)(2,1)S(1)}, bf16[5,128,1536]{2,1,0:T(8,128)(2,1)}, u32[]{:S(2)}) %copy-start.1) | copy-done | bytes 1966104
  57.3 0.0 copy-start.2
  57.3 1.1 %copy-done.2 = bf16[5,128,512]{2,1,0:T(8,128)(2,1)S(1)} copy-done((bf16[5,128,512]{2,1,0:T(8,128)(2,1)S(1)}, bf16[5,128,512]{2,1,0:T(8,128)(2,1)}, u32[]{:S(2)}) %copy-start.2) | copy-done | bytes 655384
  58.4 0.0 copy-start.3
  58.4 1.1 %copy-done.3 = bf16[5,128,512]{2,1,0:T(8,128)(2,1)S(1)} copy-done((bf16[5,128,512]{2,1,0:T(8,128)(2,1)S(1)}, bf16[5,128,512]{2,1,0:T(8,128)(2,1)}, u32[]{:S(2)}) %copy-start.3) | copy-done | bytes 655384
  59.5 0.0 copy-start.4
  59.5 1.1 %copy-done.4 = bf16[5,128,512]{2,1,0:T(8,128)(2,1)S(1)} copy-done((bf16[5,128,512]{2,1,0:T(8,128)(2,1)S(1)}, bf16[5,128,512]{2,1,0:T(8,128)(2,1)}, u32[]{:S(2)}) %copy-start.4) | copy-done | bytes 655384
  60.6 0.0 copy-start.5
  60.6 0.9 %copy-done.5 = bf16[32,1536]{1,0:T(8,128)(2,1)S(1)} copy-done((bf16[32,1536]{1,0:T(8,128)(2,1)S(1)}, bf16[32,1536]{1,0:T(8,128)(2,1)}, u32[]{:S(2)}) %copy-start.5) | copy-done | bytes 98328
  61.5 0.0 copy-start.6
  61.5 0.9 %copy-done.6 = bf16[32,1536]{1,0:T(8,128)(2,1)S(1)} copy-done((bf16[32,1536]{1,0:T(8,128)(2,1)S(1)}, bf16[32,1536]{1,0:T(8,128)(2,1)}, u32[]{:S(2)}) %copy-start.6) | copy-done | bytes 98328
  62.4 0.0 copy-start.7
  62.4 0.7 copy-done.7
  63.1 10.6 %weight_grads.1 = (bf16[5,1536,512]{2,1,0:T(8,128)(2,1)}, bf16[5,1536,512]{2,1,0:T(8,128)(2,1)}, bf16[5,512,1536]{2,1,0:T(8,128)(2,1)}, bf16[32,1536]{1,0:T(8,12...) custom-call(bf16[5,128,1536]{2,1,0:T(8,128)(2,1)S(1)} %copy-done, bf16[5,128,1536]{2,1,0:T(8,128)(2,1)S(1)} %copy-done.1, ...), custom_call_target="tpu_custom_call" | custom-call | tf_op jit(solution)/shard_map/weight_grads/pallas_call | solution.py:382
  73.7 0.7 copy.17
Async XLA Ops:
  54.2 1.5 %copy-start = (bf16[5,128,1536]{2,1,0:T(8,128)(2,1)S(1)}, bf16[5,128,1536]{2,1,0:T(8,128)(2,1)}, u32[]{:S(2)}) copy-start(bf16[5,128,1536]{2,1,0:T(8,128)(2,1)} %get-tuple-element.20.r_ref) | copy-start | bytes 5898244
  55.8 1.5 %copy-start.1 = (bf16[5,128,1536]{2,1,0:T(8,128)(2,1)S(1)}, bf16[5,128,1536]{2,1,0:T(8,128)(2,1)}, u32[]{:S(2)}) copy-start(bf16[5,128,1536]{2,1,0:T(8,128)(2,1)} %get-tuple-element.21.dy_ref) | copy-start | bytes 5898244
  57.3 1.1 %copy-start.2 = (bf16[5,128,512]{2,1,0:T(8,128)(2,1)S(1)}, bf16[5,128,512]{2,1,0:T(8,128)(2,1)}, u32[]{:S(2)}) copy-start(bf16[5,128,512]{2,1,0:T(8,128)(2,1)} %get-tuple-element.22.h_ref) | copy-start | bytes 1966084
  58.4 1.1 %copy-start.3 = (bf16[5,128,512]{2,1,0:T(8,128)(2,1)S(1)}, bf16[5,128,512]{2,1,0:T(8,128)(2,1)}, u32[]{:S(2)}) copy-start(bf16[5,128,512]{2,1,0:T(8,128)(2,1)} %get-tuple-element.23.da_ref) | copy-start | bytes 1966084
  59.5 1.1 %copy-start.4 = (bf16[5,128,512]{2,1,0:T(8,128)(2,1)S(1)}, bf16[5,128,512]{2,1,0:T(8,128)(2,1)}, u32[]{:S(2)}) copy-start(bf16[5,128,512]{2,1,0:T(8,128)(2,1)} %get-tuple-element.24.db_ref) | copy-start | bytes 1966084
  60.6 0.9 %copy-start.5 = (bf16[32,1536]{1,0:T(8,128)(2,1)S(1)}, bf16[32,1536]{1,0:T(8,128)(2,1)}, u32[]{:S(2)}) copy-start(bf16[32,1536]{1,0:T(8,128)(2,1)} %get-tuple-element.25.o_in) | copy-start | bytes 294916
  61.5 0.9 %copy-start.6 = (bf16[32,1536]{1,0:T(8,128)(2,1)S(1)}, bf16[32,1536]{1,0:T(8,128)(2,1)}, u32[]{:S(2)}) copy-start(bf16[32,1536]{1,0:T(8,128)(2,1)} %get-tuple-element.26.gx_in) | copy-start | bytes 294916
  62.4 0.7 copy-start.7

commit v2 on v1

--- a/solution.py
+++ b/solution.py
@@ -31,7 +31,7 @@
 
 def moe_kernel(dims, x_hbm, g_hbm, idx_ref, slot_ref, gate_ref, w1_hbm, w3_hbm, w2_hbm,
                out_ref, gx_ref, gg_ref, r_hbm, dy_hbm, h_hbm, da_hbm, db_hbm,
-               w1, w3, w2, xg, meta, scr, scr2, r_all, dy_all, h_all, da_all, db_all, c1_all, c2_all,
+               w1, w3, w2, xg, meta, scr, r_all, dy_all, h_all, da_all, db_all, c1_all, c2_all,
                p_all, gs_all, y_all, dr_all, part, sibbuf, ringbuf, finbuf, ggsrc, ggbuf,
                w_sem, loc_sem, wb_sem, meta_ss, meta_rs, ag_ss, ag_rs, rt_ss, rt_rs, gg_ss, gg_rs):
     G, T, D, F, E, C, K = dims
@@ -63,14 +63,11 @@
     for cp in w_copies:
         cp.start()
 
-    off = pl.multiple_of(lax.rem(me, per_tile) * T, T)
+    off = lax.rem(me, per_tile) * T
     scr[...] = jnp.zeros_like(scr)
-    scr2[...] = jnp.zeros_like(scr2)
-    code = jnp.where(slot_ref[...] >= 0, idx_ref[...] * C + slot_ref[...] + 1, 0)
-    scr[pl.ds(off, T), 0:K] = code.astype(F32)
-    scr2[pl.ds(off, T), 0:K] = gate_ref[...]
-    meta[me, 0:K] = jnp.transpose(scr[...])[0:K]
-    meta[me, K:2 * K] = jnp.transpose(scr2[...])[0:K]
+    scr[0:K, 0:T] = jnp.where(slot_ref[...] >= 0, idx_ref[...] * C + slot_ref[...] + 1, 0).astype(F32)
+    scr[K:2 * K, 0:T] = gate_ref[...]
+    meta[me] = pltpu.roll(scr[...], off, 1)
 
     barrier = pltpu.get_barrier_semaphore()
     for d in range(1, G):
@@ -306,9 +303,7 @@
     for d in range(1, G):
         gg_sends[d - 1].wait_recv()
         tot = tot + ggbuf[d - 1]
-    scr[0:K, :] = tot
-    scr2[...] = jnp.transpose(scr[...])
-    gg_ref[...] = scr2[pl.ds(off, T), 0:K]
+    gg_ref[...] = pltpu.roll(tot, lax.rem(LANES - off, LANES), 1)[:, 0:T]
     ret_2(1)
     for cp in meta_sends + sx + sg + gg_sends:
         cp.wait_send()
@@ -352,7 +347,7 @@
         aspec = pl.BlockSpec(memory_space=ANY)
         out, gx, gg, r, dy, h, da, db = pl.pallas_call(
             functools.partial(moe_kernel, dims),
-            out_shape=(sds((T, D), BF16), sds((T, D), BF16), sds((T, K), F32),
+            out_shape=(sds((T, D), BF16), sds((T, D), BF16), sds((K, T), F32),
                        sds((E, RW, D), BF16), sds((E, RW, D), BF16),
                        sds((E, RW, F), BF16), sds((E, RW, F), BF16), sds((E, RW, F), BF16)),
             in_specs=[aspec, aspec, vspec, vspec, vspec, aspec, aspec, aspec],
@@ -360,7 +355,7 @@
             scratch_shapes=[
                 vm((E, D, F), BF16), vm((E, D, F), BF16), vm((E, F, D), BF16),
                 vm((2, NT, D), BF16), vm((G, 2 * K, LANES), F32),
-                vm((LANES, LANES), F32), vm((LANES, LANES), F32),
+                vm((2 * K, LANES), F32),
                 vm((E, RW, D), BF16), vm((E, RW, D), BF16),
                 vm((E, RW, F), BF16), vm((E, RW, F), BF16), vm((E, RW, F), BF16),
                 vm((E, RW, F), F32), vm((E, RW, F), F32),
@@ -375,7 +370,7 @@
             compiler_params=pltpu.CompilerParams(
                 collective_id=0, has_side_effects=True, vmem_limit_bytes=60 * 2 ** 20),
             name="moe_exchange",
-        )(x_rows, grad_out, expert_idx, slot_pos, gate_w, w_gate, w_up, w_down)
+        )(x_rows, grad_out, expert_idx.T, slot_pos.T, gate_w.T, w_gate, w_up, w_down)
 
         blk = lambda *s: pl.BlockSpec((pl.Squeezed(),) + s, lambda e: (e,) + (0,) * len(s))
         whole = lambda *s: pl.BlockSpec(s, lambda e: (0,) * len(s))
@@ -383,14 +378,14 @@
             wgrad_kernel,
             grid=(E,),
             out_shape=(sds((E, D, F), BF16), sds((E, D, F), BF16), sds((E, F, D), BF16),
-                       sds((T, D), BF16), sds((T, D), BF16), sds((T, K), F32)),
+                       sds((T, D), BF16), sds((T, D), BF16), sds((K, T), F32)),
             in_specs=[blk(RW, D), blk(RW, D), blk(RW, F), blk(RW, F), blk(RW, F),
-                      whole(T, D), whole(T, D), whole(T, K)],
-            out_specs=(blk(D, F), blk(D, F), blk(F, D), whole(T, D), whole(T, D), whole(T, K)),
-            compiler_params=pltpu.CompilerParams(vmem_limit_bytes=40 * 2 ** 20),
+                      whole(T, D), whole(T, D), whole(K, T)],
+            out_specs=(blk(D, F), blk(D, F), blk(F, D), whole(T, D), whole(T, D), whole(K, T)),
+            compiler_params=pltpu.CompilerParams(vmem_limit_bytes=62 * 2 ** 20),
             name="weight_grads",
         )(r, dy, h, da, db, out, gx, gg)
-        return out, gx, g1, g3, g2, gg
+        return out, gx, g1, g3, g2, gg.T
 
     return jax.shard_map(per_device, mesh=mesh,
                          in_specs=(row_spec, row_spec, row_spec, row_spec, expert_spec, expert_spec, expert_spec, row_spec),

time: 75 us -> 62.9 us (0.84)
  local copies, waits for them, and re-layouts: 13.6 us -> 0 us
  Pallas kernels: 60.1 us -> 62 us
    unnamed x20 -> x0, local copies, waits for them, and re-layouts: 13.6 us -> none
    pallas_call x1, Pallas kernels: 10.6 us -> 12.4 us  [per_device(): pl.pallas_call(wgrad_kernel, grid=(E,), out_shape=(sds((E, D, F), BF16),...]
where the time goes in v2:
time: 62.9 us; the launch traced here: 62.6 us
  Pallas kernels  62 us (99%)
  between operations  0.64 us (1%)
    pallas_call x1, Pallas kernels, per_device(): pl.pallas_call(functools.partial(moe_kernel, dims), out_shape=(sds((T, D)...  49.6 us
    pallas_call x1, Pallas kernels, per_device(): pl.pallas_call(wgrad_kernel, grid=(E,), out_shape=(sds((E, D, F), BF16),...  12.4 us

profile of v2, /device:TPU:120, one launch (start us, length us, event | category | flops | bytes accessed | tf_op | source)
XLA Modules:
  0.0 62.6 jit_solution(9036825901211287366)
XLA Ops:
  0.6 49.6 %moe_exchange.1 = (bf16[32,1536]{1,0:T(8,128)(2,1)}, bf16[32,1536]{1,0:T(8,128)(2,1)}, f32[8,32]{1,0:T(8,128)}, bf16[5,128,1536]{2,1,0:T(8,128)(2,1)}, bf16[5,12...) custom-call(bf16[32,1536]{1,0:T(8,128)(2,1)} %x_hbm.1, ...), custom_call_target="tpu_custom_call" | custom-call | tf_op jit(solution)/shard_map/moe_exchange/pallas_call | solution.py:348
  50.2 12.4 %weight_grads.1 = (bf16[5,1536,512]{2,1,0:T(8,128)(2,1)}, bf16[5,1536,512]{2,1,0:T(8,128)(2,1)}, bf16[5,512,1536]{2,1,0:T(8,128)(2,1)}, bf16[32,1536]{1,0:T(8,12...) custom-call(bf16[5,128,1536]{2,1,0:T(8,128)(2,1)} %get-tuple-element.20.r_ref, ...), custom_call_target="tpu_custom_call" | custom-call | tf_op jit(solution)/shard_map/weight_grads/pallas_call | solution.py:377

commit v3 on v0

v3 whole, which is shorter than its diff:
```python
import functools

import jax
import jax.numpy as jnp
from jax import lax
from jax.experimental import pallas as pl
from jax.experimental.pallas import tpu as pltpu
from jax.sharding import PartitionSpec as P

BF16, F32 = jnp.bfloat16, jnp.float32
MESH_ID = pl.DeviceIdType.MESH
LANES = 128
N_CHUNK = 2


def capacity_of(tok_dev, top_k, n_experts):
    return ((2 * tok_dev * top_k + n_experts - 1) // n_experts + 7) // 8 * 8


def dot_nn(a, b):
    return lax.dot_general(a, b, (((1,), (0,)), ((), ())), preferred_element_type=F32)


def dot_nt(a, b):
    return lax.dot_general(a, b, (((1,), (1,)), ((), ())), preferred_element_type=F32)


def dot_tn(a, b):
    return lax.dot_general(a, b, (((0,), (0,)), ((), ())), preferred_element_type=F32)


def moe_kernel(dims, x_hbm, g_hbm, idx_hbm, slot_hbm, gate_hbm, w1_hbm, w3_hbm, w2_hbm,
               w1, w3, w2, out_ref, gx_ref, gg_ref,
               xg, meta, idx_v, slot_v, gate_v, scr, r_all, dy_all, h_all, dab_all, c1_all, c2_all,
               p_all, gs_all, y_all, dr_all, part, sibbuf, ringbuf, finbuf, ggsrc, ggbuf,
               w_sem, loc_sem, meta_ss, meta_rs, ag_ss, ag_rs, rt_ss, rt_rs, gg_ss, gg_rs):
    G, T, D, F, E, C, K = dims
    NQ = G // 2
    RW, NT = G * C, G * T
    CW = D // N_CHUNK
    per_tile = LANES // T
    me = lax.axis_index("ep")
    core = lax.rem(me, 2)
    chip = me // 2
    right_chip, left_chip, opp_chip = (lax.rem(chip + 1, NQ), lax.rem(chip + NQ - 1, NQ), lax.rem(chip + 2, NQ))
    dev = lambda q, c: q * 2 + c
    other = 1 - core
    sib = dev(chip, other)
    right, left, opp = dev(right_chip, core), dev(left_chip, core), dev(opp_chip, core)

    def rows(d):
        return pl.ds(pl.multiple_of(d * T, T), T)

    def remote(src, dst, ss, rs, target):
        return pltpu.make_async_remote_copy(src_ref=src, dst_ref=dst, send_sem=ss, recv_sem=rs,
                                            device_id={"ep": target}, device_id_type=MESH_ID)

    local = [pltpu.make_async_copy(src, dst, loc_sem.at[i]) for i, (src, dst) in enumerate((
        (idx_hbm, idx_v), (slot_hbm, slot_v), (gate_hbm, gate_v),
        (x_hbm, xg.at[0, rows(me)]), (g_hbm, xg.at[1, rows(me)])))]
    barrier = pltpu.get_barrier_semaphore()
    for d in (sib, right, left):
        pl.semaphore_signal(barrier, inc=1, device_id={"ep": d}, device_id_type=MESH_ID)
    scr[...] = jnp.zeros_like(scr)
    for cp in local:
        cp.start()
    for cp in local[:3]:
        cp.wait()
    off = lax.rem(me, per_tile) * T
    scr[0, :, 0:T] = jnp.where(slot_v[...] >= 0, idx_v[...] * C + slot_v[...] + 1, 0).astype(F32)
    scr[1, :, 0:T] = gate_v[...]
    meta[me, 0:K] = pltpu.roll(scr[0], off, 1)
    meta[me, K:2 * K] = pltpu.roll(scr[1], off, 1)
    local[3].wait()
    local[4].wait()
    w_copies = [pltpu.make_async_copy(src.at[e], dst.at[e], w_sem.at[k, e]) for e in range(E)
                for k, (src, dst) in enumerate(((w1_hbm, w1), (w3_hbm, w3), (w2_hbm, w2)))]
    for cp in w_copies:
        cp.start()
    pl.semaphore_wait(barrier, 3)

    lo, hi, full = pl.ds(0, D // 2), pl.ds(D // 2, D // 2), pl.ds(0, D)
    sib_right, sib_left, sib_opp = dev(right_chip, other), dev(left_chip, other), dev(opp_chip, other)
    ag_out = ((me, full, sib), (me, lo, right), (me, hi, right), (me, hi, left), (me, lo, left),
              (left, lo, right), (right, hi, left), (left, full, sib), (right, full, sib),
              (opp, lo, sib), (opp, hi, sib))
    ag_in = ((sib, full, sib), (left, lo, left), (left, hi, left), (right, hi, right), (right, lo, right),
             (opp, lo, left), (opp, hi, right), (sib_left, full, sib), (sib_right, full, sib),
             (sib_opp, lo, sib), (sib_opp, hi, sib))
    meta_out = ((me, sib), (me, right), (me, left), (left, right), (left, sib), (right, sib), (opp, sib))
    meta_in = ((sib, sib), (left, left), (right, right), (opp, left), (sib_left, sib), (sib_right, sib), (sib_opp, sib))

    def ag(table, t, k):
        src_dev, cols, target = table[k]
        ref = xg.at[t, rows(src_dev), cols]
        return remote(ref, ref, ag_ss.at[t, k], ag_rs.at[t, k], target)

    def mt(table, k):
        src_dev, target = table[k]
        return remote(meta.at[src_dev], meta.at[src_dev], meta_ss.at[k], meta_rs.at[k], target)

    def ag_send(t, *ks):
        for k in ks:
            ag(ag_out, t, k).start()

    def ag_recv(t, *ks):
        for k in ks:
            ag(ag_in, t, k).wait_recv()

    def mt_send(*ks):
        for k in ks:
            mt(meta_out, k).start()

    def mt_recv(*ks):
        for k in ks:
            mt(meta_in, k).wait_recv()

    ag_send(0, 1, 3)
    mt_send(1, 2, 0)
    ag_send(0, 2, 4, 0)
    ag_recv(0, 1)
    ag_send(0, 5)
    ag_recv(0, 3)
    ag_send(0, 6)
    mt_recv(1)
    mt_send(3, 4)
    mt_recv(2)
    mt_send(5)
    ag_send(1, 1, 3, 2, 4, 0)
    ag_recv(0, 2)
    ag_send(0, 7)
    ag_recv(0, 4)
    ag_send(0, 8)
    mt_recv(3)
    mt_send(6)
    ag_recv(0, 5)
    ag_send(0, 9)
    ag_recv(0, 6)
    ag_send(0, 10)
    mt_recv(0, 4, 5, 6)

    n_tiles = G // per_tile
    halves = []
    for i in range(n_tiles):
        tot = meta[i * per_tile]
        for s in range(i * per_tile + 1, (i + 1) * per_tile):
            tot = tot + meta[s]
        halves.append(tot)
    codes = jnp.concatenate([v[0:K] for v in halves], axis=1)
    gates = jnp.concatenate([v[K:2 * K] for v in halves], axis=1)
    lane_src = (lax.broadcasted_iota(jnp.int32, (K, NT), 1) // T * C).astype(F32)
    row_id = lax.broadcasted_iota(jnp.int32, (RW, NT), 0).astype(F32) + 1.0

    def routing(e):
        first = ((me * E + e) * C).astype(F32) + 1.0
        sel = (codes >= first) & (codes < first + float(C))
        pos = jnp.sum(jnp.where(sel, codes - first + lane_src + 1.0, 0.0), axis=0, keepdims=True)
        gate_row = jnp.sum(jnp.where(sel, gates, 0.0), axis=0, keepdims=True)
        return sel, row_id == pos, gate_row

    def erow(e):
        return pl.ds(e * RW, RW)

    for e in range(E):
        sel, mask, gate_row = routing(e)
        p_all[erow(e), :] = jnp.where(mask, 1.0, 0.0).astype(BF16)
        rest = gate_row
        for i in range(3):
            piece = rest.astype(BF16).astype(F32)
            gs_all[i, erow(e), :] = jnp.where(mask, piece, 0.0).astype(BF16)
            rest = rest - piece

    ag_recv(0, 0, 7, 8, 9, 10)
    ag_recv(1, 1)
    ag_send(1, 5)
    ag_recv(1, 3)
    ag_send(1, 6)
    for cp in w_copies:
        cp.wait()

    def select_x(e):
        r_all[e] = dot_nn(p_all[erow(e), :], xg[0]).astype(BF16)

    def up(e):
        a = dot_nn(r_all[e], w1[e])
        b = dot_nn(r_all[e], w3[e])
        s = jax.nn.sigmoid(a)
        act = a * s
        h_all[e] = (act * b).astype(BF16)
        c1_all[e] = b * (s * (1.0 + a * (1.0 - s)))
        c2_all[e] = act

    def down(e):
        y_all[erow(e), :] = dot_nn(h_all[e], w2[e]).astype(BF16)

    select_x(0)
    for e in range(E):
        if e + 1 < E:
            select_x(e + 1)
        up(e)
        if e > 0:
            down(e - 1)
        if e == 2:
            ag_recv(1, 2)
            ag_send(1, 7)
            ag_recv(1, 4)
            ag_send(1, 8)
    down(E - 1)
    ag_recv(1, 5)
    ag_send(1, 9)
    ag_recv(1, 6)
    ag_send(1, 10)

    chips = (opp_chip, right_chip, left_chip, chip)
    HW = CW // 2

    def cols(j):
        return pl.ds(j * CW, CW)

    def half(j, i):
        return pl.ds(j * CW + i * HW, HW)

    c_half = (pl.ds(0, HW), pl.ds(HW, HW))

    def ret_desc(t, j, n):
        u = t * N_CHUNK + j
        if n < 4:
            src, dst, tgt = part.at[t, rows(dev(chips[n], other)), cols(j)], sibbuf.at[u, n], sib
        elif n == 4:
            src, dst, tgt = part.at[t, rows(opp), half(j, 0)], ringbuf.at[u, 0], right
        elif n == 5:
            src, dst, tgt = part.at[t, rows(opp), half(j, 1)], ringbuf.at[u, 1], left
        elif n in (6, 8):
            i = 1 if n == 6 else 0
            src, dst, tgt = part.at[t, rows(right), half(j, i)], finbuf.at[u, 0, :, c_half[i]], right
        else:
            i = 0 if n == 7 else 1
            src, dst, tgt = part.at[t, rows(left), half(j, i)], finbuf.at[u, 1, :, c_half[i]], left
        return remote(src, dst, rt_ss.at[u, n], rt_rs.at[u, n], tgt)

    def ret_0(t, j):
        for n in range(4):
            ret_desc(t, j, n).start()

    def ret_1(t, j):
        u = t * N_CHUNK + j
        for n, d in enumerate((opp, right, left, me)):
            ret_desc(t, j, n).wait_recv()
            part[t, rows(d), cols(j)] += sibbuf[u, n]
            for m in ((4, 5), (6,), (7,), ())[n]:
                ret_desc(t, j, m).start()

    def ret_2(t, j):
        u = t * N_CHUNK + j
        for n, d, i in ((4, right, 0), (5, left, 1)):
            ret_desc(t, j, n).wait_recv()
            part[t, rows(d), half(j, i)] += ringbuf[u, i]
            ret_desc(t, j, n + 4).start()

    def ret_3(t, j, res_ref):
        u = t * N_CHUNK + j
        for n in (6, 7, 8, 9):
            ret_desc(t, j, n).wait_recv()
        res_ref[:, cols(j)] = (part[t, rows(me), cols(j)] + finbuf[u, 0] + finbuf[u, 1]).astype(BF16)

    for j in range(N_CHUNK):
        acc = dot_tn(gs_all[0], y_all[:, cols(j)])
        for i in (1, 2):
            acc = acc + dot_tn(gs_all[i], y_all[:, cols(j)])
        part[0, :, cols(j)] = acc
        ret_0(0, j)

    ag_recv(1, 0, 7, 8, 9, 10)

    gg = jnp.zeros((K, NT), F32)

    def select_g(e, gg):
        sel, mask, gate_row = routing(e)
        gate_col = jnp.sum(jnp.where(mask, gate_row, 0.0), axis=1, keepdims=True)
        g_e = dot_nn(p_all[erow(e), :], xg[1])
        dy_all[e] = (gate_col * g_e).astype(BF16)
        gg_col = jnp.sum(g_e * y_all[erow(e), :].astype(F32), axis=1, keepdims=True)
        gg_row = jnp.sum(jnp.where(mask, gg_col, 0.0), axis=0, keepdims=True)
        return gg + jnp.where(sel, gg_row, 0.0)

    def down_t(e):
        dh = dot_nt(dy_all[e], w2[e])
        dab_all[e, :, 0:F] = (dh * c1_all[e]).astype(BF16)
        dab_all[e, :, F:2 * F] = (dh * c2_all[e]).astype(BF16)

    gg = select_g(0, gg)
    for e in range(E):
        if e + 1 < E:
            gg = select_g(e + 1, gg)
        down_t(e)
        if e == 1:
            ret_1(0, 0)
            ret_1(0, 1)
    for i in range(n_tiles):
        ggsrc[i] = gg[:, i * LANES:(i + 1) * LANES]

    def gg_desc(d):
        tgt = lax.rem(me + d, G)
        return remote(ggsrc.at[tgt // per_tile], ggbuf.at[d - 1], gg_ss.at[d - 1], gg_rs.at[d - 1], tgt)

    for j in range(N_CHUNK):
        for e in range(E):
            dr_all[erow(e), cols(j)] = (dot_nt(dab_all[e, :, 0:F], w1[e, cols(j), :])
                                        + dot_nt(dab_all[e, :, F:2 * F], w3[e, cols(j), :])).astype(BF16)
            if e == 1 and j == 0:
                ret_2(0, 0)
                ret_2(0, 1)
            if e == 2 and j > 0:
                ret_1(1, j - 1)
        part[1, :, cols(j)] = dot_tn(p_all[...], dr_all[:, cols(j)])
        ret_0(1, j)

    for d in range(1, G):
        gg_desc(d).start()

    def wgrad(e):
        step = D // 6
        for m in range(6):
            sl = pl.ds(m * step, step)
            res = dot_tn(r_all[e, :, sl], dab_all[e])
            w1[e, sl, :] = res[:, 0:F].astype(BF16)
            w3[e, sl, :] = res[:, F:2 * F].astype(BF16)
        for m in range(2):
            sl = pl.ds(m * (F // 2), F // 2)
            w2[e, sl, :] = dot_tn(h_all[e, :, sl], dy_all[e]).astype(BF16)

    ret_2(1, 0)
    for j in range(N_CHUNK):
        ret_3(0, j, out_ref)
    ret_1(1, N_CHUNK - 1)
    wgrad(0)
    tot = ggsrc[me // per_tile]
    for d in range(1, G):
        gg_desc(d).wait_recv()
        tot = tot + ggbuf[d - 1]
    gg_ref[...] = pltpu.roll(tot, lax.rem(LANES - off, LANES), 1)[:, 0:T]
    wgrad(1)
    ret_2(1, N_CHUNK - 1)
    for e in range(2, E):
        wgrad(e)
    for j in range(N_CHUNK):
        ret_3(1, j, gx_ref)
    for k in range(len(meta_out)):
        mt(meta_out, k).wait_send()
    for t in range(2):
        for k in range(len(ag_out)):
            ag(ag_out, t, k).wait_send()
        for j in range(N_CHUNK):
            for n in range(10):
                ret_desc(t, j, n).wait_send()
    for d in range(1, G):
        gg_desc(d).wait_send()


def write_kernel(n_exp, *refs):
    n = 6
    src, dst, sem = refs[:n], refs[n:2 * n], refs[2 * n]
    copies = []
    for e in range(n_exp):
        for k in range(3):
            copies.append(pltpu.make_async_copy(src[k].at[e], dst[k].at[e], sem.at[k, e]))
    for k in range(3, n):
        copies.append(pltpu.make_async_copy(src[k], dst[k], sem.at[k, 0]))
    for cp in copies:
        cp.start()
    for cp in copies:
        cp.wait()


def solution(mesh):
    group_size = mesh.shape['ep']
    row_spec = P(('dp', 'ep'))
    expert_spec = P('ep')

    def per_device(x_rows, expert_idx, gate_w, slot_pos, w_gate, w_up, w_down, grad_out):
        T, D = x_rows.shape
        K = expert_idx.shape[1]
        E, _, F = w_gate.shape
        G = group_size
        C = capacity_of(T, K, E * G)
        RW, NT = G * C, G * T
        NQ = G // 2
        CW = D // N_CHUNK
        dims = (G, T, D, F, E, C, K)
        vm = pltpu.VMEM
        dma = pltpu.SemaphoreType.DMA
        vspec = pl.BlockSpec(memory_space=pltpu.VMEM)
        aspec = pl.BlockSpec(memory_space=pl.ANY)
        results = [((E, D, F), BF16), ((E, D, F), BF16), ((E, F, D), BF16), ((T, D), BF16), ((T, D), BF16), ((K, T), F32)]
        held = pl.pallas_call(
            functools.partial(moe_kernel, dims),
            out_shape=[vm(*r) for r in results],
            in_specs=[aspec] * 8,
            out_specs=[vspec] * len(results),
            scratch_shapes=[
                vm((2, NT, D), BF16), vm((G, 2 * K, LANES), F32), vm((K, T), jnp.int32), vm((K, T), jnp.int32), vm((K, T), F32),
                vm((2, K, LANES), F32),
                vm((E, RW, D), BF16), vm((E, RW, D), BF16),
                vm((E, RW, F), BF16), vm((E, RW, 2 * F), BF16),
                vm((E, RW, F), F32), vm((E, RW, F), F32),
                vm((E * RW, NT), BF16), vm((3, E * RW, NT), BF16),
                vm((E * RW, D), BF16), vm((E * RW, D), BF16),
                vm((2, NT, D), F32), vm((2 * N_CHUNK, NQ, T, CW), F32),
                vm((2 * N_CHUNK, 2, T, CW // 2), F32), vm((2 * N_CHUNK, 2, T, CW), F32),
                vm((NT // LANES, K, LANES), F32), vm((G - 1, K, LANES), F32),
                dma((3, E)), dma((5,)), dma((7,)), dma((7,)),
                dma((2, 11)), dma((2, 11)), dma((2 * N_CHUNK, 10)), dma((2 * N_CHUNK, 10)),
                dma((G - 1,)), dma((G - 1,)),
            ],
            compiler_params=pltpu.CompilerParams(
                collective_id=0, has_side_effects=True, vmem_limit_bytes=36 * 2 ** 20),
            name="moe_exchange",
        )(x_rows, grad_out, expert_idx.T, slot_pos.T, gate_w.T, w_gate, w_up, w_down)
        g1, g3, g2, out, gx, gg = pl.pallas_call(
            functools.partial(write_kernel, E),
            out_shape=[jax.ShapeDtypeStruct(*r) for r in results],
            in_specs=[vspec] * len(results),
            out_specs=[aspec] * len(results),
            scratch_shapes=[dma((len(results), E))],
            compiler_params=pltpu.CompilerParams(vmem_limit_bytes=2 ** 20),
            name="write_results",
        )(*held)
        return out, gx, g1, g3, g2, gg.T

    return jax.shard_map(per_device, mesh=mesh,
                         in_specs=(row_spec, row_spec, row_spec, row_spec, expert_spec, expert_spec, expert_spec, row_spec),
                         out_specs=(row_spec, row_spec, row_spec, row_spec, row_spec, row_spec),
                         check_vma=False)
```

time: 154 us -> 53.7 us (0.35)
  waiting for transfers between devices: 55.5 us -> 0 us
  Pallas kernels: 0 us -> 52.8 us
  matrix products: 47.8 us -> 0 us
  local copies, waits for them, and re-layouts: 22.2 us -> 0 us
  starting transfers between devices: 18.1 us -> 0 us
  other arithmetic: 8.18 us -> 0 us
    all_to_all x4 -> x0, waiting for transfers between devices: 55.5 us -> none  [the longest x1 19.6 us: per_device(): recv_x = lax.all_to_all(send_x, 'ep', 0, 0, tiled=True)]
    pallas_call x0 -> x2, Pallas kernels: none -> 52.8 us  [the longest x1 44.6 us: per_device(): pl.pallas_call(functools.partial(moe_kernel, dims), out_shape=[vm(*r) for...]
    dot_general x10 -> x0, matrix products: 47.8 us -> none  [the longest x1 7.02 us: per_device(): jnp.einsum('secd,secf->edf', recv_x, d_gate, preferred_element_type=jnp.f...]
    all_to_all x4 -> x0, starting transfers between devices: 18.1 us -> none  [the longest x1 4.74 us: per_device(): lax.all_to_all(d_rows, 'ep', 0, 0, tiled=True).reshape(n_rows, model_dim)]
    gather x5 -> x0, local copies, waits for them, and re-layouts: 16.1 us -> none  [take_rows(): return jnp.take(table, where_from, axis=0, mode='fill', fill_value=0)]
    select_n x6 -> x0, other arithmetic: 3.79 us -> none  [the longest x4 3.04 us: take_rows(): return jnp.take(table, where_from, axis=0, mode='fill', fill_value=0)]
    convert_element_type x2 -> x0, local copies, waits for them, and re-layouts: 2.83 us -> none  [the longest x1 1.43 us: per_device(): (jnp.einsum('secf,edf->secd', d_gate, w_gate, preferred_element_type=jnp....]
    reduce_sum x2 -> x0, other arithmetic: 2.55 us -> none  [the longest x1 1.48 us: per_device(): jnp.sum(gate_w[:, :, None] * y_choice.astype(jnp.float32), axis=1)]
  transfers between devices with their start and end apart: 4 -> 0, of which waited for: 4 -> 0; matrix products, arithmetic and copies ran while one was open for 30% -> 0% of each run, Pallas kernels for 0% -> 0%
where the time goes in v3:
time: 53.7 us; the launch traced here: 53.6 us
  Pallas kernels  52.8 us (98%)
  between operations  0.8 us (1%)
    pallas_call x1, Pallas kernels, per_device(): pl.pallas_call(functools.partial(moe_kernel, dims), out_shape=[vm(*r) for...  44.6 us
    pallas_call x1, Pallas kernels, per_device(): pl.pallas_call(functools.partial(write_kernel, E), out_shape=[jax.ShapeDt...  8.17 us

profile of v3, /device:TPU:120, one launch (start us, length us, event | category | flops | bytes accessed | tf_op | source)
XLA Modules:
  0.0 53.6 jit_solution(18014497685729826710)
XLA Ops:
  0.6 44.6 %moe_exchange.1 = (bf16[5,1536,512]{2,1,0:T(8,128)(2,1)S(1)}, bf16[5,1536,512]{2,1,0:T(8,128)(2,1)S(1)}, bf16[5,512,1536]{2,1,0:T(8,128)(2,1)S(1)}, bf16[32,1536...) custom-call(bf16[32,1536]{1,0:T(8,128)(2,1)} %x_hbm.1, bf16[32,1536]{1,0:T(8,128)(2,1)} %g_hbm.1, ...), custom_call_target="tpu_custom_call" | custom-call | tf_op jit(solution)/shard_map/moe_exchange/pallas_call | solution.py:395
  45.2 8.2 %write_results.1 = (bf16[5,1536,512]{2,1,0:T(8,128)(2,1)}, bf16[5,1536,512]{2,1,0:T(8,128)(2,1)}, bf16[5,512,1536]{2,1,0:T(8,128)(2,1)}, bf16[32,1536]{1,0:T(8,1...) custom-call(bf16[5,1536,512]{2,1,0:T(8,128)(2,1)S(1)} %get-tuple-element.18.refs_0_, ...), custom_call_target="tpu_custom_call" | custom-call | tf_op jit(solution)/shard_map/write_results/pallas_call | solution.py:419

commit v4 on v3

--- a/solution.py
+++ b/solution.py
@@ -11,6 +11,8 @@
 MESH_ID = pl.DeviceIdType.MESH
 LANES = 128
 N_CHUNK = 2
+TB = 256
+EARLY = 3
 
 
 def capacity_of(tok_dev, top_k, n_experts):
@@ -29,10 +31,19 @@
     return lax.dot_general(a, b, (((0,), (0,)), ((), ())), preferred_element_type=F32)
 
 
+def up_grads(r, dab, e, g1, g3, n):
+    D, F = r.shape[2], dab.shape[2] // 2
+    for m in range(0, D, TB):
+        sl = pl.ds(m, TB)
+        res = dot_tn(r[e, :, sl], dab[e])
+        g1[n, sl, :] = res[:, 0:F].astype(BF16)
+        g3[n, sl, :] = res[:, F:2 * F].astype(BF16)
+
+
 def moe_kernel(dims, x_hbm, g_hbm, idx_hbm, slot_hbm, gate_hbm, w1_hbm, w3_hbm, w2_hbm,
-               w1, w3, w2, out_ref, gx_ref, gg_ref,
-               xg, meta, idx_v, slot_v, gate_v, scr, r_all, dy_all, h_all, dab_all, c1_all, c2_all,
-               p_all, gs_all, y_all, dr_all, part, sibbuf, ringbuf, finbuf, ggsrc, ggbuf,
+               w1, w3, r_all, dy_all, h_all, dab_all, out_ref, gx_ref, gg_ref,
+               w2, w13t, xg, meta, idx_v, slot_v, gate_v, scr, tok, c1_all, c2_all,
+               p_all, comb, y_all, part, sibbuf, ringbuf, finbuf, ggsrc, ggbuf,
                w_sem, loc_sem, meta_ss, meta_rs, ag_ss, ag_rs, rt_ss, rt_rs, gg_ss, gg_rs):
     G, T, D, F, E, C, K = dims
     NQ = G // 2
@@ -118,6 +129,30 @@
     ag_send(0, 1, 3)
     mt_send(1, 2, 0)
     ag_send(0, 2, 4, 0)
+    def wait_w(k, e):
+        w_copies[e * 3 + k].wait()
+
+    def flip_up(e):
+        wait_w(0, e)
+        wait_w(1, e)
+        for k, w in enumerate((w1, w3)):
+            for i in range(0, D, TB):
+                for j in range(0, F, TB):
+                    w13t[e, pl.ds(k * F + j, TB), pl.ds(i, TB)] = w[e, pl.ds(i, TB), pl.ds(j, TB)].T
+
+    def flip_down(e):
+        for b in range(0, D, F):
+            for i in range(0, F, TB):
+                for j in range(i, F, TB):
+                    up_ref = w2.at[e, pl.ds(i, TB), pl.ds(b + j, TB)]
+                    low_ref = w2.at[e, pl.ds(j, TB), pl.ds(b + i, TB)]
+                    up_t, low_t = up_ref[...].T, low_ref[...].T
+                    up_ref[...] = low_t
+                    if i != j:
+                        low_ref[...] = up_t
+
+    flip_up(0)
+    flip_up(1)
     ag_recv(0, 1)
     ag_send(0, 5)
     ag_recv(0, 3)
@@ -127,12 +162,15 @@
     mt_recv(2)
     mt_send(5)
     ag_send(1, 1, 3, 2, 4, 0)
+    flip_up(2)
     ag_recv(0, 2)
     ag_send(0, 7)
     ag_recv(0, 4)
     ag_send(0, 8)
     mt_recv(3)
     mt_send(6)
+    flip_up(3)
+    flip_up(4)
     ag_recv(0, 5)
     ag_send(0, 9)
     ag_recv(0, 6)
@@ -162,21 +200,32 @@
         return pl.ds(e * RW, RW)
 
     for e in range(E):
-        sel, mask, gate_row = routing(e)
-        p_all[erow(e), :] = jnp.where(mask, 1.0, 0.0).astype(BF16)
-        rest = gate_row
-        for i in range(3):
-            piece = rest.astype(BF16).astype(F32)
-            gs_all[i, erow(e), :] = jnp.where(mask, piece, 0.0).astype(BF16)
-            rest = rest - piece
+        p_all[erow(e), :] = jnp.where(routing(e)[1], 1.0, 0.0).astype(BF16)
+
+    EC = E * C
+    tok[...] = jnp.transpose(jnp.concatenate([codes, gates], axis=0))
+    pair = lax.broadcasted_iota(jnp.int32, (NT, LANES), 1)
+    want = jnp.where(pair < EC, pair + me * EC + 1, -1).astype(F32)
+    one, rest = jnp.zeros((NT, LANES), F32), jnp.zeros((NT, LANES), F32)
+    for k in range(K):
+        hit = tok[:, k:k + 1] == want
+        one = jnp.where(hit, 1.0, one)
+        rest = jnp.where(hit, tok[:, K + k:K + k + 1], rest)
+    for i in range(3):
+        piece = rest.astype(BF16)
+        for s in range(G):
+            comb[s, pl.ds(i * T, T), :] = piece[s * T:(s + 1) * T]
+        rest = rest - piece.astype(F32)
+    for s in range(G):
+        comb[s, pl.ds(3 * T, T), :] = one[s * T:(s + 1) * T].astype(BF16)
 
     ag_recv(0, 0, 7, 8, 9, 10)
     ag_recv(1, 1)
     ag_send(1, 5)
     ag_recv(1, 3)
     ag_send(1, 6)
-    for cp in w_copies:
-        cp.wait()
+    for e in range(E):
+        wait_w(2, e)
 
     def select_x(e):
         r_all[e] = dot_nn(p_all[erow(e), :], xg[0]).astype(BF16)
@@ -190,26 +239,16 @@
         c1_all[e] = b * (s * (1.0 + a * (1.0 - s)))
         c2_all[e] = act
 
-    def down(e):
-        y_all[erow(e), :] = dot_nn(h_all[e], w2[e]).astype(BF16)
-
     select_x(0)
     for e in range(E):
         if e + 1 < E:
             select_x(e + 1)
         up(e)
-        if e > 0:
-            down(e - 1)
         if e == 2:
             ag_recv(1, 2)
             ag_send(1, 7)
             ag_recv(1, 4)
             ag_send(1, 8)
-    down(E - 1)
-    ag_recv(1, 5)
-    ag_send(1, 9)
-    ag_recv(1, 6)
-    ag_send(1, 10)
 
     chips = (opp_chip, right_chip, left_chip, chip)
     HW = CW // 2
@@ -263,12 +302,22 @@
             ret_desc(t, j, n).wait_recv()
         res_ref[:, cols(j)] = (part[t, rows(me), cols(j)] + finbuf[u, 0] + finbuf[u, 1]).astype(BF16)
 
+    def put_rows(e, j, val):
+        for s in range(G):
+            y_all[s, pl.ds(e * C, C), cols(j)] = val[s * C:(s + 1) * C]
+
     for j in range(N_CHUNK):
-        acc = dot_tn(gs_all[0], y_all[:, cols(j)])
-        for i in (1, 2):
-            acc = acc + dot_tn(gs_all[i], y_all[:, cols(j)])
-        part[0, :, cols(j)] = acc
+        for e in range(E):
+            put_rows(e, j, dot_nn(h_all[e], w2[e, :, cols(j)]).astype(BF16))
+        for s in range(G):
+            acc = dot_nn(comb[s, 0:3 * T, 0:EC], y_all[s, :, cols(j)])
+            part[0, pl.ds(s * T, T), cols(j)] = acc[0:T] + acc[T:2 * T] + acc[2 * T:3 * T]
         ret_0(0, j)
+        if j == 0:
+            ag_recv(1, 5)
+            ag_send(1, 9)
+            ag_recv(1, 6)
+            ag_send(1, 10)
 
     ag_recv(1, 0, 7, 8, 9, 10)
 
@@ -279,21 +328,26 @@
         gate_col = jnp.sum(jnp.where(mask, gate_row, 0.0), axis=1, keepdims=True)
         g_e = dot_nn(p_all[erow(e), :], xg[1])
         dy_all[e] = (gate_col * g_e).astype(BF16)
-        gg_col = jnp.sum(g_e * y_all[erow(e), :].astype(F32), axis=1, keepdims=True)
+        y_e = y_all[:, pl.ds(e * C, C), :].reshape(RW, D)
+        gg_col = jnp.sum(g_e * y_e.astype(F32), axis=1, keepdims=True)
         gg_row = jnp.sum(jnp.where(mask, gg_col, 0.0), axis=0, keepdims=True)
         return gg + jnp.where(sel, gg_row, 0.0)
 
     def down_t(e):
-        dh = dot_nt(dy_all[e], w2[e])
+        dh = dot_nn(dy_all[e, :, 0:F], w2[e, :, 0:F])
+        for b in range(F, D, F):
+            dh = dh + dot_nn(dy_all[e, :, b:b + F], w2[e, :, b:b + F])
         dab_all[e, :, 0:F] = (dh * c1_all[e]).astype(BF16)
         dab_all[e, :, F:2 * F] = (dh * c2_all[e]).astype(BF16)
 
+    flip_down(0)
     gg = select_g(0, gg)
     for e in range(E):
         if e + 1 < E:
+            flip_down(e + 1)
             gg = select_g(e + 1, gg)
         down_t(e)
-        if e == 1:
+        if e == 2:
             ret_1(0, 0)
             ret_1(0, 1)
     for i in range(n_tiles):
@@ -305,44 +359,33 @@
 
     for j in range(N_CHUNK):
         for e in range(E):
-            dr_all[erow(e), cols(j)] = (dot_nt(dab_all[e, :, 0:F], w1[e, cols(j), :])
-                                        + dot_nt(dab_all[e, :, F:2 * F], w3[e, cols(j), :])).astype(BF16)
-            if e == 1 and j == 0:
-                ret_2(0, 0)
-                ret_2(0, 1)
+            put_rows(e, j, dot_nn(dab_all[e], w13t[e, :, cols(j)]).astype(BF16))
             if e == 2 and j > 0:
                 ret_1(1, j - 1)
-        part[1, :, cols(j)] = dot_tn(p_all[...], dr_all[:, cols(j)])
+        for s in range(G):
+            part[1, pl.ds(s * T, T), cols(j)] = dot_nn(comb[s, 3 * T:4 * T, 0:EC], y_all[s, :, cols(j)])
         ret_0(1, j)
+        if j == 0:
+            ret_2(0, 0)
+            ret_2(0, 1)
 
     for d in range(1, G):
         gg_desc(d).start()
-
-    def wgrad(e):
-        step = D // 6
-        for m in range(6):
-            sl = pl.ds(m * step, step)
-            res = dot_tn(r_all[e, :, sl], dab_all[e])
-            w1[e, sl, :] = res[:, 0:F].astype(BF16)
-            w3[e, sl, :] = res[:, F:2 * F].astype(BF16)
-        for m in range(2):
-            sl = pl.ds(m * (F // 2), F // 2)
-            w2[e, sl, :] = dot_tn(h_all[e, :, sl], dy_all[e]).astype(BF16)
 
     ret_2(1, 0)
     for j in range(N_CHUNK):
         ret_3(0, j, out_ref)
     ret_1(1, N_CHUNK - 1)
-    wgrad(0)
+    up_grads(r_all, dab_all, 0, w1, w3, 0)
     tot = ggsrc[me // per_tile]
     for d in range(1, G):
         gg_desc(d).wait_recv()
         tot = tot + ggbuf[d - 1]
     gg_ref[...] = pltpu.roll(tot, lax.rem(LANES - off, LANES), 1)[:, 0:T]
-    wgrad(1)
+    up_grads(r_all, dab_all, 1, w1, w3, 1)
     ret_2(1, N_CHUNK - 1)
-    for e in range(2, E):
-        wgrad(e)
+    for e in range(2, EARLY):
+        up_grads(r_all, dab_all, e, w1, w3, e)
     for j in range(N_CHUNK):
         ret_3(1, j, gx_ref)
     for k in range(len(meta_out)):
@@ -357,17 +400,29 @@
         gg_desc(d).wait_send()
 
 
-def write_kernel(n_exp, *refs):
-    n = 6
-    src, dst, sem = refs[:n], refs[n:2 * n], refs[2 * n]
+def write_kernel(n_exp, g1, g3, r, dy, h, dab, out, gx, gg, g1_hbm, g3_hbm, g2_hbm, out_hbm, gx_hbm, gg_hbm,
+                 late1, late3, g2, sem, small_sem):
     copies = []
+
+    def send(src, dst, s):
+        copies.append(pltpu.make_async_copy(src, dst, s))
+        copies[-1].start()
+
+    for e in range(EARLY):
+        send(g1.at[e], g1_hbm.at[e], sem.at[0, e])
+        send(g3.at[e], g3_hbm.at[e], sem.at[1, e])
+    for k, (src, dst) in enumerate(((out, out_hbm), (gx, gx_hbm), (gg, gg_hbm))):
+        send(src, dst, small_sem.at[k])
+    F = h.shape[2]
     for e in range(n_exp):
-        for k in range(3):
-            copies.append(pltpu.make_async_copy(src[k].at[e], dst[k].at[e], sem.at[k, e]))
-    for k in range(3, n):
-        copies.append(pltpu.make_async_copy(src[k], dst[k], sem.at[k, 0]))
-    for cp in copies:
-        cp.start()
+        for m in range(0, F, TB):
+            g2[e, pl.ds(m, TB), :] = dot_tn(h[e, :, pl.ds(m, TB)], dy[e]).astype(BF16)
+        send(g2.at[e], g2_hbm.at[e], sem.at[2, e])
+        if e >= EARLY:
+            n = e - EARLY
+            up_grads(r, dab, e, late1, late3, n)
+            send(late1.at[n], g1_hbm.at[e], sem.at[0, e])
+            send(late3.at[n], g3_hbm.at[e], sem.at[1, e])
     for cp in copies:
         cp.wait()
 
@@ -391,38 +446,43 @@
         dma = pltpu.SemaphoreType.DMA
         vspec = pl.BlockSpec(memory_space=pltpu.VMEM)
         aspec = pl.BlockSpec(memory_space=pl.ANY)
-        results = [((E, D, F), BF16), ((E, D, F), BF16), ((E, F, D), BF16), ((T, D), BF16), ((T, D), BF16), ((K, T), F32)]
+        small = [((T, D), BF16), ((T, D), BF16), ((K, T), F32)]
+        held_shapes = [((E, D, F), BF16), ((E, D, F), BF16), ((E, RW, D), BF16), ((E, RW, D), BF16),
+                       ((E, RW, F), BF16), ((E, RW, 2 * F), BF16)] + small
+        results = [((E, D, F), BF16), ((E, D, F), BF16), ((E, F, D), BF16)] + small
+        n_units = 2 * N_CHUNK
         held = pl.pallas_call(
             functools.partial(moe_kernel, dims),
-            out_shape=[vm(*r) for r in results],
+            out_shape=[vm(*r) for r in held_shapes],
             in_specs=[aspec] * 8,
-            out_specs=[vspec] * len(results),
+            out_specs=[vspec] * len(held_shapes),
             scratch_shapes=[
-                vm((2, NT, D), BF16), vm((G, 2 * K, LANES), F32), vm((K, T), jnp.int32), vm((K, T), jnp.int32), vm((K, T), F32),
-                vm((2, K, LANES), F32),
-                vm((E, RW, D), BF16), vm((E, RW, D), BF16),
-                vm((E, RW, F), BF16), vm((E, RW, 2 * F), BF16),
+                vm((E, F, D), BF16), vm((E, 2 * F, D), BF16),
+                vm((2, NT, D), BF16), vm((G, 2 * K, LANES), F32),
+                vm((K, T), jnp.int32), vm((K, T), jnp.int32), vm((K, T), F32),
+                vm((2, K, LANES), F32), vm((NT, 2 * K), F32),
                 vm((E, RW, F), F32), vm((E, RW, F), F32),
-                vm((E * RW, NT), BF16), vm((3, E * RW, NT), BF16),
-                vm((E * RW, D), BF16), vm((E * RW, D), BF16),
-                vm((2, NT, D), F32), vm((2 * N_CHUNK, NQ, T, CW), F32),
-                vm((2 * N_CHUNK, 2, T, CW // 2), F32), vm((2 * N_CHUNK, 2, T, CW), F32),
+                vm((E * RW, NT), BF16), vm((G, 4 * T, LANES), BF16),
+                vm((G, E * C, D), BF16),
+                vm((2, NT, D), F32), vm((n_units, NQ, T, CW), F32),
+                vm((n_units, 2, T, CW // 2), F32), vm((n_units, 2, T, CW), F32),
                 vm((NT // LANES, K, LANES), F32), vm((G - 1, K, LANES), F32),
                 dma((3, E)), dma((5,)), dma((7,)), dma((7,)),
-                dma((2, 11)), dma((2, 11)), dma((2 * N_CHUNK, 10)), dma((2 * N_CHUNK, 10)),
+                dma((2, 11)), dma((2, 11)), dma((n_units, 10)), dma((n_units, 10)),
                 dma((G - 1,)), dma((G - 1,)),
             ],
             compiler_params=pltpu.CompilerParams(
-                collective_id=0, has_side_effects=True, vmem_limit_bytes=36 * 2 ** 20),
+                collective_id=0, has_side_effects=True, vmem_limit_bytes=39 * 2 ** 20),
             name="moe_exchange",
         )(x_rows, grad_out, expert_idx.T, slot_pos.T, gate_w.T, w_gate, w_up, w_down)
         g1, g3, g2, out, gx, gg = pl.pallas_call(
             functools.partial(write_kernel, E),
             out_shape=[jax.ShapeDtypeStruct(*r) for r in results],
-            in_specs=[vspec] * len(results),
+            in_specs=[vspec] * len(held_shapes),
             out_specs=[aspec] * len(results),
-            scratch_shapes=[dma((len(results), E))],
-            compiler_params=pltpu.CompilerParams(vmem_limit_bytes=2 ** 20),
+            scratch_shapes=[vm((E - EARLY, D, F), BF16), vm((E - EARLY, D, F), BF16), vm((E, F, D), BF16),
+                            dma((3, E)), dma((len(small),))],
+            compiler_params=pltpu.CompilerParams(vmem_limit_bytes=16 * 2 ** 20),
             name="write_results",
         )(*held)
         return out, gx, g1, g3, g2, gg.T

time: 53.7 us -> 50.8 us (0.946)
  Pallas kernels: 52.8 us -> 49.9 us
    pallas_call x1, Pallas kernels: 44.6 us -> 41.8 us  [per_device(): pl.pallas_call(functools.partial(moe_kernel, dims), out_shape=[vm(*r) for...]
where the time goes in v4:
time: 50.8 us; the launch traced here: 50.7 us
  Pallas kernels  49.9 us (98%)
  between operations  0.8 us (2%)
    pallas_call x1, Pallas kernels, per_device(): pl.pallas_call(functools.partial(moe_kernel, dims), out_shape=[vm(*r) for...  41.8 us
    pallas_call x1, Pallas kernels, per_device(): pl.pallas_call(functools.partial(write_kernel, E), out_shape=[jax.ShapeDt...  8.14 us

profile of v4, /device:TPU:120, one launch (start us, length us, event | category | flops | bytes accessed | tf_op | source)
XLA Modules:
  0.0 50.7 jit_solution(7813643680402543568)
XLA Ops:
  0.6 41.8 %moe_exchange.1 = (bf16[5,1536,512]{2,1,0:T(8,128)(2,1)S(1)}, bf16[5,1536,512]{2,1,0:T(8,128)(2,1)S(1)}, bf16[5,128,1536]{2,1,0:T(8,128)(2,1)S(1)}, bf16[5,128,1...) custom-call(bf16[32,1536]{1,0:T(8,128)(2,1)} %x_hbm.1, ...), custom_call_target="tpu_custom_call" | custom-call | tf_op jit(solution)/shard_map/moe_exchange/pallas_call | solution.py:454
  42.4 8.1 %write_results.1 = (bf16[5,1536,512]{2,1,0:T(8,128)(2,1)}, bf16[5,1536,512]{2,1,0:T(8,128)(2,1)}, bf16[5,512,1536]{2,1,0:T(8,128)(2,1)}, bf16[32,1536]{1,0:T(8,1...) custom-call(bf16[5,1536,512]{2,1,0:T(8,128)(2,1)S(1)} %get-tuple-element.21.g1, ...), custom_call_target="tpu_custom_call" | custom-call | tf_op jit(solution)/shard_map/write_results/pallas_call | solution.py:478

commit v5 on v4

--- a/solution.py
+++ b/solution.py
@@ -10,9 +10,9 @@
 BF16, F32 = jnp.bfloat16, jnp.float32
 MESH_ID = pl.DeviceIdType.MESH
 LANES = 128
-N_CHUNK = 2
+N_CHUNK = 3
 TB = 256
-EARLY = 3
+EARLY = 4
 
 
 def capacity_of(tok_dev, top_k, n_experts):
@@ -42,13 +42,14 @@
 
 def moe_kernel(dims, x_hbm, g_hbm, idx_hbm, slot_hbm, gate_hbm, w1_hbm, w3_hbm, w2_hbm,
                w1, w3, r_all, dy_all, h_all, dab_all, out_ref, gx_ref, gg_ref,
-               w2, w13t, xg, meta, idx_v, slot_v, gate_v, scr, tok, c1_all, c2_all,
+               w2, w1t, w2t, xg, meta, idx_v, slot_v, gate_v, scr, tok, c1_all, c2_all,
                p_all, comb, y_all, part, sibbuf, ringbuf, finbuf, ggsrc, ggbuf,
-               w_sem, loc_sem, meta_ss, meta_rs, ag_ss, ag_rs, rt_ss, rt_rs, gg_ss, gg_rs):
+               w_sem, loc_sem, meta_ss, meta_rs, ag_ss, ag_rs, rt_ss, rt_rs, gg_sem):
     G, T, D, F, E, C, K = dims
     NQ = G // 2
     RW, NT = G * C, G * T
     CW = D // N_CHUNK
+    assert CW == F and G == 8
     per_tile = LANES // T
     me = lax.axis_index("ep")
     core = lax.rem(me, 2)
@@ -69,6 +70,10 @@
     local = [pltpu.make_async_copy(src, dst, loc_sem.at[i]) for i, (src, dst) in enumerate((
         (idx_hbm, idx_v), (slot_hbm, slot_v), (gate_hbm, gate_v),
         (x_hbm, xg.at[0, rows(me)]), (g_hbm, xg.at[1, rows(me)])))]
+
+    def wait_bytes(ref, sem):
+        pltpu.make_async_copy(ref, ref, sem).wait()
+
     barrier = pltpu.get_barrier_semaphore()
     for d in (sib, right, left):
         pl.semaphore_signal(barrier, inc=1, device_id={"ep": d}, device_id_type=MESH_ID)
@@ -84,10 +89,11 @@
     meta[me, K:2 * K] = pltpu.roll(scr[1], off, 1)
     local[3].wait()
     local[4].wait()
-    w_copies = [pltpu.make_async_copy(src.at[e], dst.at[e], w_sem.at[k, e]) for e in range(E)
-                for k, (src, dst) in enumerate(((w1_hbm, w1), (w3_hbm, w3), (w2_hbm, w2)))]
-    for cp in w_copies:
-        cp.start()
+    for e in range(E):
+        pltpu.make_async_copy(w1_hbm.at[e], w1.at[e], w_sem.at[e]).start()
+        pltpu.make_async_copy(w2_hbm.at[e], w2.at[e], w_sem.at[e]).start()
+    for e in range(E):
+        pltpu.make_async_copy(w3_hbm.at[e], w3.at[e], w_sem.at[E]).start()
     pl.semaphore_wait(barrier, 3)
 
     lo, hi, full = pl.ds(0, D // 2), pl.ds(D // 2, D // 2), pl.ds(0, D)
@@ -104,11 +110,11 @@
     def ag(table, t, k):
         src_dev, cols, target = table[k]
         ref = xg.at[t, rows(src_dev), cols]
-        return remote(ref, ref, ag_ss.at[t, k], ag_rs.at[t, k], target)
+        return remote(ref, ref, ag_ss.at[t], ag_rs.at[t, k if k < 7 else 0], target)
 
     def mt(table, k):
         src_dev, target = table[k]
-        return remote(meta.at[src_dev], meta.at[src_dev], meta_ss.at[k], meta_rs.at[k], target)
+        return remote(meta.at[src_dev], meta.at[src_dev], meta_ss, meta_rs.at[k if k < 4 else 0], target)
 
     def ag_send(t, *ks):
         for k in ks:
@@ -118,6 +124,9 @@
         for k in ks:
             ag(ag_in, t, k).wait_recv()
 
+    def ag_recv_sib(t):
+        wait_bytes(xg.at[t, pl.ds(0, NQ * T)], ag_rs.at[t, 0])
+
     def mt_send(*ks):
         for k in ks:
             mt(meta_out, k).start()
@@ -129,30 +138,29 @@
     ag_send(0, 1, 3)
     mt_send(1, 2, 0)
     ag_send(0, 2, 4, 0)
-    def wait_w(k, e):
-        w_copies[e * 3 + k].wait()
-
-    def flip_up(e):
-        wait_w(0, e)
-        wait_w(1, e)
-        for k, w in enumerate((w1, w3)):
-            for i in range(0, D, TB):
-                for j in range(0, F, TB):
-                    w13t[e, pl.ds(k * F + j, TB), pl.ds(i, TB)] = w[e, pl.ds(i, TB), pl.ds(j, TB)].T
-
-    def flip_down(e):
+
+    def flip(dst, src):
+        for i in range(0, src.shape[0], TB):
+            for j in range(0, src.shape[1], TB):
+                dst[pl.ds(j, TB), pl.ds(i, TB)] = src[pl.ds(i, TB), pl.ds(j, TB)].T
+
+    def flip_12(e):
+        wait_bytes(w1.at[pl.ds(0, 2)], w_sem.at[e])
+        flip(w1t.at[e], w1.at[e])
+        flip(w2t.at[e], w2.at[e])
+
+    def flip_3(e):
         for b in range(0, D, F):
             for i in range(0, F, TB):
                 for j in range(i, F, TB):
-                    up_ref = w2.at[e, pl.ds(i, TB), pl.ds(b + j, TB)]
-                    low_ref = w2.at[e, pl.ds(j, TB), pl.ds(b + i, TB)]
+                    up_ref = w3.at[e, pl.ds(b + i, TB), pl.ds(j, TB)]
+                    low_ref = w3.at[e, pl.ds(b + j, TB), pl.ds(i, TB)]
                     up_t, low_t = up_ref[...].T, low_ref[...].T
                     up_ref[...] = low_t
                     if i != j:
                         low_ref[...] = up_t
 
-    flip_up(0)
-    flip_up(1)
+    flip_12(0)
     ag_recv(0, 1)
     ag_send(0, 5)
     ag_recv(0, 3)
@@ -162,20 +170,21 @@
     mt_recv(2)
     mt_send(5)
     ag_send(1, 1, 3, 2, 4, 0)
-    flip_up(2)
+    flip_12(1)
+    flip_12(2)
     ag_recv(0, 2)
     ag_send(0, 7)
     ag_recv(0, 4)
     ag_send(0, 8)
     mt_recv(3)
     mt_send(6)
-    flip_up(3)
-    flip_up(4)
+    flip_12(3)
     ag_recv(0, 5)
     ag_send(0, 9)
     ag_recv(0, 6)
     ag_send(0, 10)
-    mt_recv(0, 4, 5, 6)
+    flip_12(E - 1)
+    wait_bytes(meta.at[pl.ds(0, NQ)], meta_rs.at[0])
 
     n_tiles = G // per_tile
     halves = []
@@ -203,29 +212,31 @@
         p_all[erow(e), :] = jnp.where(routing(e)[1], 1.0, 0.0).astype(BF16)
 
     EC = E * C
-    tok[...] = jnp.transpose(jnp.concatenate([codes, gates], axis=0))
-    pair = lax.broadcasted_iota(jnp.int32, (NT, LANES), 1)
-    want = jnp.where(pair < EC, pair + me * EC + 1, -1).astype(F32)
-    one, rest = jnp.zeros((NT, LANES), F32), jnp.zeros((NT, LANES), F32)
-    for k in range(K):
-        hit = tok[:, k:k + 1] == want
-        one = jnp.where(hit, 1.0, one)
-        rest = jnp.where(hit, tok[:, K + k:K + k + 1], rest)
-    for i in range(3):
-        piece = rest.astype(BF16)
+
+    def build_comb():
+        tok[...] = jnp.transpose(jnp.concatenate([codes, gates], axis=0))
+        pair = lax.broadcasted_iota(jnp.int32, (NT, LANES), 1)
+        want = jnp.where(pair < EC, pair + me * EC + 1, -1).astype(F32)
+        one, rest = jnp.zeros((NT, LANES), F32), jnp.zeros((NT, LANES), F32)
+        for k in range(K):
+            hit = tok[:, k:k + 1] == want
+            one = jnp.where(hit, 1.0, one)
+            rest = jnp.where(hit, tok[:, K + k:K + k + 1], rest)
+        for i in range(3):
+            piece = rest.astype(BF16)
+            for s in range(G):
+                comb[s, pl.ds(i * T, T), :] = piece[s * T:(s + 1) * T]
+            rest = rest - piece.astype(F32)
         for s in range(G):
-            comb[s, pl.ds(i * T, T), :] = piece[s * T:(s + 1) * T]
-        rest = rest - piece.astype(F32)
-    for s in range(G):
-        comb[s, pl.ds(3 * T, T), :] = one[s * T:(s + 1) * T].astype(BF16)
-
-    ag_recv(0, 0, 7, 8, 9, 10)
+            comb[s, pl.ds(3 * T, T), :] = one[s * T:(s + 1) * T].astype(BF16)
+
+    ag_recv_sib(0)
+    wait_bytes(w3, w_sem.at[E])
+
     ag_recv(1, 1)
     ag_send(1, 5)
     ag_recv(1, 3)
     ag_send(1, 6)
-    for e in range(E):
-        wait_w(2, e)
 
     def select_x(e):
         r_all[e] = dot_nn(p_all[erow(e), :], xg[0]).astype(BF16)
@@ -244,6 +255,9 @@
         if e + 1 < E:
             select_x(e + 1)
         up(e)
+        flip_3(e)
+        if e == 0:
+            build_comb()
         if e == 2:
             ag_recv(1, 2)
             ag_send(1, 7)
@@ -275,7 +289,7 @@
         else:
             i = 0 if n == 7 else 1
             src, dst, tgt = part.at[t, rows(left), half(j, i)], finbuf.at[u, 1, :, c_half[i]], left
-        return remote(src, dst, rt_ss.at[u, n], rt_rs.at[u, n], tgt)
+        return remote(src, dst, rt_ss, rt_rs.at[u, (0, 0, 0, 0, 1, 2, 3, 4, 3, 4)[n]], tgt)
 
     def ret_0(t, j):
         for n in range(4):
@@ -283,8 +297,8 @@
 
     def ret_1(t, j):
         u = t * N_CHUNK + j
+        wait_bytes(sibbuf.at[u], rt_rs.at[u, 0])
         for n, d in enumerate((opp, right, left, me)):
-            ret_desc(t, j, n).wait_recv()
             part[t, rows(d), cols(j)] += sibbuf[u, n]
             for m in ((4, 5), (6,), (7,), ())[n]:
                 ret_desc(t, j, m).start()
@@ -298,8 +312,8 @@
 
     def ret_3(t, j, res_ref):
         u = t * N_CHUNK + j
-        for n in (6, 7, 8, 9):
-            ret_desc(t, j, n).wait_recv()
+        wait_bytes(finbuf.at[u, 0], rt_rs.at[u, 3])
+        wait_bytes(finbuf.at[u, 1], rt_rs.at[u, 4])
         res_ref[:, cols(j)] = (part[t, rows(me), cols(j)] + finbuf[u, 0] + finbuf[u, 1]).astype(BF16)
 
     def put_rows(e, j, val):
@@ -319,7 +333,7 @@
             ag_recv(1, 6)
             ag_send(1, 10)
 
-    ag_recv(1, 0, 7, 8, 9, 10)
+    ag_recv_sib(1)
 
     gg = jnp.zeros((K, NT), F32)
 
@@ -334,97 +348,87 @@
         return gg + jnp.where(sel, gg_row, 0.0)
 
     def down_t(e):
-        dh = dot_nn(dy_all[e, :, 0:F], w2[e, :, 0:F])
-        for b in range(F, D, F):
-            dh = dh + dot_nn(dy_all[e, :, b:b + F], w2[e, :, b:b + F])
+        dh = dot_nn(dy_all[e], w2t[e])
         dab_all[e, :, 0:F] = (dh * c1_all[e]).astype(BF16)
         dab_all[e, :, F:2 * F] = (dh * c2_all[e]).astype(BF16)
 
-    flip_down(0)
     gg = select_g(0, gg)
     for e in range(E):
         if e + 1 < E:
-            flip_down(e + 1)
             gg = select_g(e + 1, gg)
         down_t(e)
-        if e == 2:
-            ret_1(0, 0)
-            ret_1(0, 1)
+        if e < N_CHUNK:
+            ret_1(0, e)
     for i in range(n_tiles):
         ggsrc[i] = gg[:, i * LANES:(i + 1) * LANES]
 
     def gg_desc(d):
         tgt = lax.rem(me + d, G)
-        return remote(ggsrc.at[tgt // per_tile], ggbuf.at[d - 1], gg_ss.at[d - 1], gg_rs.at[d - 1], tgt)
+        return remote(ggsrc.at[tgt // per_tile], ggbuf.at[d - 1], gg_sem.at[0], gg_sem.at[1], tgt)
 
     for j in range(N_CHUNK):
         for e in range(E):
-            put_rows(e, j, dot_nn(dab_all[e], w13t[e, :, cols(j)]).astype(BF16))
-            if e == 2 and j > 0:
-                ret_1(1, j - 1)
+            dr = dot_nn(dab_all[e, :, 0:F], w1t[e, :, cols(j)]) + dot_nn(dab_all[e, :, F:2 * F], w3[e, cols(j), :])
+            put_rows(e, j, dr.astype(BF16))
+        if j == 2:
+            ret_1(1, 0)
         for s in range(G):
             part[1, pl.ds(s * T, T), cols(j)] = dot_nn(comb[s, 3 * T:4 * T, 0:EC], y_all[s, :, cols(j)])
         ret_0(1, j)
-        if j == 0:
-            ret_2(0, 0)
-            ret_2(0, 1)
+        ret_2(0, j)
 
     for d in range(1, G):
         gg_desc(d).start()
 
+    ret_1(1, 1)
+    up_grads(r_all, dab_all, 0, w1, w3, 0)
+    ret_1(1, 2)
+    up_grads(r_all, dab_all, 1, w1, w3, 1)
     ret_2(1, 0)
+    ret_2(1, 1)
+    up_grads(r_all, dab_all, 2, w1, w3, 2)
+    ret_2(1, 2)
     for j in range(N_CHUNK):
         ret_3(0, j, out_ref)
-    ret_1(1, N_CHUNK - 1)
-    up_grads(r_all, dab_all, 0, w1, w3, 0)
+    for e in range(3, EARLY):
+        up_grads(r_all, dab_all, e, w1, w3, e)
     tot = ggsrc[me // per_tile]
+    wait_bytes(ggbuf, gg_sem.at[1])
     for d in range(1, G):
-        gg_desc(d).wait_recv()
         tot = tot + ggbuf[d - 1]
     gg_ref[...] = pltpu.roll(tot, lax.rem(LANES - off, LANES), 1)[:, 0:T]
-    up_grads(r_all, dab_all, 1, w1, w3, 1)
-    ret_2(1, N_CHUNK - 1)
-    for e in range(2, EARLY):
-        up_grads(r_all, dab_all, e, w1, w3, e)
     for j in range(N_CHUNK):
         ret_3(1, j, gx_ref)
-    for k in range(len(meta_out)):
-        mt(meta_out, k).wait_send()
-    for t in range(2):
-        for k in range(len(ag_out)):
-            ag(ag_out, t, k).wait_send()
-        for j in range(N_CHUNK):
-            for n in range(10):
-                ret_desc(t, j, n).wait_send()
-    for d in range(1, G):
-        gg_desc(d).wait_send()
+    sent = pl.ds(0, (G - 1) * T)
+    wait_bytes(meta.at[pl.ds(0, G - 1)], meta_ss)
+    wait_bytes(xg.at[0, sent], ag_ss.at[0])
+    wait_bytes(xg.at[1, sent], ag_ss.at[1])
+    wait_bytes(ggbuf, gg_sem.at[0])
+    wait_bytes(part.at[:, sent], rt_ss)
 
 
 def write_kernel(n_exp, g1, g3, r, dy, h, dab, out, gx, gg, g1_hbm, g3_hbm, g2_hbm, out_hbm, gx_hbm, gg_hbm,
-                 late1, late3, g2, sem, small_sem):
-    copies = []
-
-    def send(src, dst, s):
-        copies.append(pltpu.make_async_copy(src, dst, s))
-        copies[-1].start()
+                 late1, late3, g2, sem):
+    def send(src, dst, k):
+        pltpu.make_async_copy(src, dst, sem.at[k]).start()
 
     for e in range(EARLY):
-        send(g1.at[e], g1_hbm.at[e], sem.at[0, e])
-        send(g3.at[e], g3_hbm.at[e], sem.at[1, e])
+        send(g1.at[e], g1_hbm.at[e], 0)
+        send(g3.at[e], g3_hbm.at[e], 1)
     for k, (src, dst) in enumerate(((out, out_hbm), (gx, gx_hbm), (gg, gg_hbm))):
-        send(src, dst, small_sem.at[k])
+        send(src, dst, 3 + k)
     F = h.shape[2]
     for e in range(n_exp):
         for m in range(0, F, TB):
             g2[e, pl.ds(m, TB), :] = dot_tn(h[e, :, pl.ds(m, TB)], dy[e]).astype(BF16)
-        send(g2.at[e], g2_hbm.at[e], sem.at[2, e])
+        send(g2.at[e], g2_hbm.at[e], 2)
         if e >= EARLY:
             n = e - EARLY
             up_grads(r, dab, e, late1, late3, n)
-            send(late1.at[n], g1_hbm.at[e], sem.at[0, e])
-            send(late3.at[n], g3_hbm.at[e], sem.at[1, e])
-    for cp in copies:
-        cp.wait()
+            send(late1.at[n], g1_hbm.at[e], 0)
+            send(late3.at[n], g3_hbm.at[e], 1)
+    for k, ref in enumerate((g1_hbm, g3_hbm, g2_hbm, out_hbm, gx_hbm, gg_hbm)):
+        pltpu.make_async_copy(ref, ref, sem.at[k]).wait()
 
 
 def solution(mesh):
@@ -457,7 +461,7 @@
             in_specs=[aspec] * 8,
             out_specs=[vspec] * len(held_shapes),
             scratch_shapes=[
-                vm((E, F, D), BF16), vm((E, 2 * F, D), BF16),
+                vm((E, F, D), BF16), vm((E, F, D), BF16), vm((E, D, F), BF16),
                 vm((2, NT, D), BF16), vm((G, 2 * K, LANES), F32),
                 vm((K, T), jnp.int32), vm((K, T), jnp.int32), vm((K, T), F32),
                 vm((2, K, LANES), F32), vm((NT, 2 * K), F32),
@@ -467,9 +471,8 @@
                 vm((2, NT, D), F32), vm((n_units, NQ, T, CW), F32),
                 vm((n_units, 2, T, CW // 2), F32), vm((n_units, 2, T, CW), F32),
                 vm((NT // LANES, K, LANES), F32), vm((G - 1, K, LANES), F32),
-                dma((3, E)), dma((5,)), dma((7,)), dma((7,)),
-                dma((2, 11)), dma((2, 11)), dma((n_units, 10)), dma((n_units, 10)),
-                dma((G - 1,)), dma((G - 1,)),
+                dma((E + 1,)), dma((5,)), dma, dma((4,)),
+                dma((2,)), dma((2, 7)), dma, dma((n_units, 5)), dma((2,)),
             ],
             compiler_params=pltpu.CompilerParams(
                 collective_id=0, has_side_effects=True, vmem_limit_bytes=39 * 2 ** 20),
@@ -481,7 +484,7 @@
             in_specs=[vspec] * len(held_shapes),
             out_specs=[aspec] * len(results),
             scratch_shapes=[vm((E - EARLY, D, F), BF16), vm((E - EARLY, D, F), BF16), vm((E, F, D), BF16),
-                            dma((3, E)), dma((len(small),))],
+                            dma((len(results),))],
             compiler_params=pltpu.CompilerParams(vmem_limit_bytes=16 * 2 ** 20),
             name="write_results",
         )(*held)

time: 50.8 us -> 45.2 us (0.89)
  Pallas kernels: 49.9 us -> 44.3 us
    pallas_call x1, Pallas kernels: 41.8 us -> 36.2 us  [per_device(): pl.pallas_call(functools.partial(moe_kernel, dims), out_shape=[vm(*r) for...]
where the time goes in v5:
time: 45.2 us; the launch traced here: 45.1 us
  Pallas kernels  44.3 us (98%)
  between operations  0.8 us (2%)
    pallas_call x1, Pallas kernels, per_device(): pl.pallas_call(functools.partial(moe_kernel, dims), out_shape=[vm(*r) for...  36.2 us
    pallas_call x1, Pallas kernels, per_device(): pl.pallas_call(functools.partial(write_kernel, E), out_shape=[jax.ShapeDt...  8.04 us

profile of v5, /device:TPU:120, one launch (start us, length us, event | category | flops | bytes accessed | tf_op | source)
XLA Modules:
  0.0 45.1 jit_solution(17261171201475401996)
XLA Ops:
  0.6 36.2 %moe_exchange.1 = (bf16[5,1536,512]{2,1,0:T(8,128)(2,1)S(1)}, bf16[5,1536,512]{2,1,0:T(8,128)(2,1)S(1)}, bf16[5,128,1536]{2,1,0:T(8,128)(2,1)S(1)}, bf16[5,128,1...) custom-call(bf16[32,1536]{1,0:T(8,128)(2,1)} %x_hbm.1, ...), custom_call_target="tpu_custom_call" | custom-call | tf_op jit(solution)/shard_map/moe_exchange/pallas_call | solution.py:458
  36.9 8.0 %write_results.1 = (bf16[5,1536,512]{2,1,0:T(8,128)(2,1)}, bf16[5,1536,512]{2,1,0:T(8,128)(2,1)}, bf16[5,512,1536]{2,1,0:T(8,128)(2,1)}, bf16[32,1536]{1,0:T(8,1...) custom-call(bf16[5,1536,512]{2,1,0:T(8,128)(2,1)S(1)} %get-tuple-element.21.g1, ...), custom_call_target="tpu_custom_call" | custom-call | tf_op jit(solution)/shard_map/write_results/pallas_call | solution.py:481

commit v6 on v5

--- a/solution.py
+++ b/solution.py
@@ -12,7 +12,8 @@
 LANES = 128
 N_CHUNK = 3
 TB = 256
-EARLY = 4
+EARLY = 2
+SLOTS = 3
 
 
 def capacity_of(tok_dev, top_k, n_experts):
@@ -41,7 +42,7 @@
 
 
 def moe_kernel(dims, x_hbm, g_hbm, idx_hbm, slot_hbm, gate_hbm, w1_hbm, w3_hbm, w2_hbm,
-               w1, w3, r_all, dy_all, h_all, dab_all, out_ref, gx_ref, gg_ref,
+               w1, w3, r_all, dy_all, h_all, dab_all, out_ref, gg_ref, own_ref, tor_ref, tol_ref,
                w2, w1t, w2t, xg, meta, idx_v, slot_v, gate_v, scr, tok, c1_all, c2_all,
                p_all, comb, y_all, part, sibbuf, ringbuf, finbuf, ggsrc, ggbuf,
                w_sem, loc_sem, meta_ss, meta_rs, ag_ss, ag_rs, rt_ss, rt_rs, gg_sem):
@@ -289,7 +290,7 @@
         else:
             i = 0 if n == 7 else 1
             src, dst, tgt = part.at[t, rows(left), half(j, i)], finbuf.at[u, 1, :, c_half[i]], left
-        return remote(src, dst, rt_ss, rt_rs.at[u, (0, 0, 0, 0, 1, 2, 3, 4, 3, 4)[n]], tgt)
+        return remote(src, dst, rt_ss.at[t], rt_rs.at[u, (0, 0, 0, 0, 1, 2, 3, 4, 3, 4)[n]], tgt)
 
     def ret_0(t, j):
         for n in range(4):
@@ -301,14 +302,22 @@
         for n, d in enumerate((opp, right, left, me)):
             part[t, rows(d), cols(j)] += sibbuf[u, n]
             for m in ((4, 5), (6,), (7,), ())[n]:
-                ret_desc(t, j, m).start()
+                if t == 0 or m < 6:
+                    ret_desc(t, j, m).start()
 
     def ret_2(t, j):
         u = t * N_CHUNK + j
         for n, d, i in ((4, right, 0), (5, left, 1)):
             ret_desc(t, j, n).wait_recv()
-            part[t, rows(d), half(j, i)] += ringbuf[u, i]
-            ret_desc(t, j, n + 4).start()
+            if t == 0:
+                part[t, rows(d), half(j, i)] += ringbuf[u, i]
+                ret_desc(t, j, n + 4).start()
+            else:
+                to_ref = (tor_ref, tol_ref)[i]
+                to_ref[:, half(j, i)] = part[t, rows(d), half(j, i)] + ringbuf[u, i]
+                to_ref[:, half(j, 1 - i)] = part[t, rows(d), half(j, 1 - i)]
+        if t == 1:
+            own_ref[:, cols(j)] = part[t, rows(me), cols(j)]
 
     def ret_3(t, j, res_ref):
         u = t * N_CHUNK + j
@@ -320,13 +329,21 @@
         for s in range(G):
             y_all[s, pl.ds(e * C, C), cols(j)] = val[s * C:(s + 1) * C]
 
-    for j in range(N_CHUNK):
+    def y_cols(j):
         for e in range(E):
             put_rows(e, j, dot_nn(h_all[e], w2[e, :, cols(j)]).astype(BF16))
+
+    def combine_y(j):
         for s in range(G):
             acc = dot_nn(comb[s, 0:3 * T, 0:EC], y_all[s, :, cols(j)])
             part[0, pl.ds(s * T, T), cols(j)] = acc[0:T] + acc[T:2 * T] + acc[2 * T:3 * T]
         ret_0(0, j)
+
+    y_cols(0)
+    for j in range(N_CHUNK):
+        if j + 1 < N_CHUNK:
+            y_cols(j + 1)
+        combine_y(j)
         if j == 0:
             ag_recv(1, 5)
             ag_send(1, 9)
@@ -352,13 +369,14 @@
         dab_all[e, :, 0:F] = (dh * c1_all[e]).astype(BF16)
         dab_all[e, :, F:2 * F] = (dh * c2_all[e]).astype(BF16)
 
+    ret_1(0, 0)
     gg = select_g(0, gg)
     for e in range(E):
         if e + 1 < E:
             gg = select_g(e + 1, gg)
         down_t(e)
-        if e < N_CHUNK:
-            ret_1(0, e)
+        if e + 1 < N_CHUNK:
+            ret_1(0, e + 1)
     for i in range(n_tiles):
         ggsrc[i] = gg[:, i * LANES:(i + 1) * LANES]
 
@@ -366,48 +384,54 @@
         tgt = lax.rem(me + d, G)
         return remote(ggsrc.at[tgt // per_tile], ggbuf.at[d - 1], gg_sem.at[0], gg_sem.at[1], tgt)
 
-    for j in range(N_CHUNK):
+    for d in range(1, G):
+        gg_desc(d).start()
+
+    def dr_cols(j):
         for e in range(E):
             dr = dot_nn(dab_all[e, :, 0:F], w1t[e, :, cols(j)]) + dot_nn(dab_all[e, :, F:2 * F], w3[e, cols(j), :])
             put_rows(e, j, dr.astype(BF16))
-        if j == 2:
-            ret_1(1, 0)
+
+    def combine_dr(j):
         for s in range(G):
             part[1, pl.ds(s * T, T), cols(j)] = dot_nn(comb[s, 3 * T:4 * T, 0:EC], y_all[s, :, cols(j)])
         ret_0(1, j)
+
+    dr_cols(0)
+    for j in range(N_CHUNK):
+        if j + 1 < N_CHUNK:
+            dr_cols(j + 1)
+        combine_dr(j)
+        if j + 1 == N_CHUNK:
+            ret_1(1, 0)
         ret_2(0, j)
 
-    for d in range(1, G):
-        gg_desc(d).start()
-
     ret_1(1, 1)
+    ret_1(1, 2)
     up_grads(r_all, dab_all, 0, w1, w3, 0)
-    ret_1(1, 2)
     up_grads(r_all, dab_all, 1, w1, w3, 1)
     ret_2(1, 0)
-    ret_2(1, 1)
-    up_grads(r_all, dab_all, 2, w1, w3, 2)
-    ret_2(1, 2)
     for j in range(N_CHUNK):
         ret_3(0, j, out_ref)
-    for e in range(3, EARLY):
+    ret_2(1, 1)
+    for e in range(2, EARLY):
         up_grads(r_all, dab_all, e, w1, w3, e)
     tot = ggsrc[me // per_tile]
     wait_bytes(ggbuf, gg_sem.at[1])
     for d in range(1, G):
         tot = tot + ggbuf[d - 1]
     gg_ref[...] = pltpu.roll(tot, lax.rem(LANES - off, LANES), 1)[:, 0:T]
-    for j in range(N_CHUNK):
-        ret_3(1, j, gx_ref)
+    ret_2(1, 2)
     sent = pl.ds(0, (G - 1) * T)
     wait_bytes(meta.at[pl.ds(0, G - 1)], meta_ss)
     wait_bytes(xg.at[0, sent], ag_ss.at[0])
     wait_bytes(xg.at[1, sent], ag_ss.at[1])
     wait_bytes(ggbuf, gg_sem.at[0])
-    wait_bytes(part.at[:, sent], rt_ss)
-
-
-def write_kernel(n_exp, g1, g3, r, dy, h, dab, out, gx, gg, g1_hbm, g3_hbm, g2_hbm, out_hbm, gx_hbm, gg_hbm,
+    wait_bytes(part.at[0, sent], rt_ss.at[0])
+    wait_bytes(part.at[1, pl.ds(0, (NQ + 1) * T)], rt_ss.at[1])
+
+
+def write_kernel(n_exp, g1, g3, r, dy, h, dab, out, gg, g1_hbm, g3_hbm, g2_hbm, out_hbm, gg_hbm,
                  late1, late3, g2, sem):
     def send(src, dst, k):
         pltpu.make_async_copy(src, dst, sem.at[k]).start()
@@ -415,20 +439,32 @@
     for e in range(EARLY):
         send(g1.at[e], g1_hbm.at[e], 0)
         send(g3.at[e], g3_hbm.at[e], 1)
-    for k, (src, dst) in enumerate(((out, out_hbm), (gx, gx_hbm), (gg, gg_hbm))):
-        send(src, dst, 3 + k)
+    send(out, out_hbm, 2)
+    send(gg, gg_hbm, 3)
     F = h.shape[2]
+
+    def down_copy(e):
+        return pltpu.make_async_copy(g2.at[e % SLOTS], g2_hbm.at[e], sem.at[4 + e % SLOTS])
+
     for e in range(n_exp):
+        if e >= SLOTS:
+            down_copy(e - SLOTS).wait()
         for m in range(0, F, TB):
-            g2[e, pl.ds(m, TB), :] = dot_tn(h[e, :, pl.ds(m, TB)], dy[e]).astype(BF16)
-        send(g2.at[e], g2_hbm.at[e], 2)
+            g2[e % SLOTS, pl.ds(m, TB), :] = dot_tn(h[e, :, pl.ds(m, TB)], dy[e]).astype(BF16)
+        down_copy(e).start()
         if e >= EARLY:
             n = e - EARLY
             up_grads(r, dab, e, late1, late3, n)
             send(late1.at[n], g1_hbm.at[e], 0)
             send(late3.at[n], g3_hbm.at[e], 1)
-    for k, ref in enumerate((g1_hbm, g3_hbm, g2_hbm, out_hbm, gx_hbm, gg_hbm)):
+    for e in range(n_exp - SLOTS, n_exp):
+        down_copy(e).wait()
+    for k, ref in enumerate((g1_hbm, g3_hbm, out_hbm, gg_hbm)):
         pltpu.make_async_copy(ref, ref, sem.at[k]).wait()
+
+
+def add_kernel(own, from_left, from_right, gx):
+    gx[...] = (own[...] + from_left[...] + from_right[...]).astype(BF16)
 
 
 def solution(mesh):
@@ -450,12 +486,13 @@
         dma = pltpu.SemaphoreType.DMA
         vspec = pl.BlockSpec(memory_space=pltpu.VMEM)
         aspec = pl.BlockSpec(memory_space=pl.ANY)
-        small = [((T, D), BF16), ((T, D), BF16), ((K, T), F32)]
+        small = [((T, D), BF16), ((K, T), F32)]
+        partial = [((T, D), F32)] * 3
         held_shapes = [((E, D, F), BF16), ((E, D, F), BF16), ((E, RW, D), BF16), ((E, RW, D), BF16),
-                       ((E, RW, F), BF16), ((E, RW, 2 * F), BF16)] + small
+                       ((E, RW, F), BF16), ((E, RW, 2 * F), BF16)] + small + partial
         results = [((E, D, F), BF16), ((E, D, F), BF16), ((E, F, D), BF16)] + small
         n_units = 2 * N_CHUNK
-        held = pl.pallas_call(
+        *held, own, to_right, to_left = pl.pallas_call(
             functools.partial(moe_kernel, dims),
             out_shape=[vm(*r) for r in held_shapes],
             in_specs=[aspec] * 8,
@@ -469,25 +506,37 @@
                 vm((E * RW, NT), BF16), vm((G, 4 * T, LANES), BF16),
                 vm((G, E * C, D), BF16),
                 vm((2, NT, D), F32), vm((n_units, NQ, T, CW), F32),
-                vm((n_units, 2, T, CW // 2), F32), vm((n_units, 2, T, CW), F32),
+                vm((n_units, 2, T, CW // 2), F32), vm((N_CHUNK, 2, T, CW), F32),
                 vm((NT // LANES, K, LANES), F32), vm((G - 1, K, LANES), F32),
                 dma((E + 1,)), dma((5,)), dma, dma((4,)),
-                dma((2,)), dma((2, 7)), dma, dma((n_units, 5)), dma((2,)),
+                dma((2,)), dma((2, 7)), dma((2,)), dma((n_units, 5)), dma((2,)),
             ],
             compiler_params=pltpu.CompilerParams(
                 collective_id=0, has_side_effects=True, vmem_limit_bytes=39 * 2 ** 20),
             name="moe_exchange",
         )(x_rows, grad_out, expert_idx.T, slot_pos.T, gate_w.T, w_gate, w_up, w_down)
-        g1, g3, g2, out, gx, gg = pl.pallas_call(
+        ahead = [(d, (d + 2) % G) for d in range(G)]
+        from_left = lax.ppermute(to_right, 'ep', ahead)
+        from_right = lax.ppermute(to_left, 'ep', [(b, a) for a, b in ahead])
+        g1, g3, g2, out, gg = pl.pallas_call(
             functools.partial(write_kernel, E),
             out_shape=[jax.ShapeDtypeStruct(*r) for r in results],
-            in_specs=[vspec] * len(held_shapes),
+            in_specs=[vspec] * len(held),
             out_specs=[aspec] * len(results),
-            scratch_shapes=[vm((E - EARLY, D, F), BF16), vm((E - EARLY, D, F), BF16), vm((E, F, D), BF16),
-                            dma((len(results),))],
-            compiler_params=pltpu.CompilerParams(vmem_limit_bytes=16 * 2 ** 20),
+            scratch_shapes=[vm((E - EARLY, D, F), BF16), vm((E - EARLY, D, F), BF16), vm((SLOTS, F, D), BF16),
+                            dma((4 + SLOTS,))],
+            compiler_params=pltpu.CompilerParams(vmem_limit_bytes=15 * 2 ** 20),
+            cost_estimate=pl.CostEstimate(flops=4 * E * RW * D * F, bytes_accessed=6 * E * D * F, transcendentals=0),
             name="write_results",
         )(*held)
+        gx = pl.pallas_call(
+            add_kernel,
+            out_shape=jax.ShapeDtypeStruct((T, D), BF16),
+            in_specs=[vspec] * 3,
+            out_specs=vspec,
+            compiler_params=pltpu.CompilerParams(vmem_limit_bytes=2 ** 21),
+            name="add_partials",
+        )(own, from_left, from_right)
         return out, gx, g1, g3, g2, gg.T
 
     return jax.shard_map(per_device, mesh=mesh,

time: 45.2 us -> 42.7 us (0.945)
  Pallas kernels: 44.3 us -> 38.6 us
  starting transfers between devices: 0 us -> 3.32 us
    pallas_call x1, Pallas kernels: 36.2 us -> 29.9 us  [per_device(): pl.pallas_call(functools.partial(moe_kernel, dims), out_shape=[vm(*r) for...]
    ppermute x0 -> x2, starting transfers between devices: none -> 3.32 us  [the longest x1 2.05 us: per_device(): from_right = lax.ppermute(to_left, 'ep', [(b, a) for a, b in ahead])]
    pallas_call x0 -> x1, Pallas kernels: none -> 0.67 us  [per_device(): pl.pallas_call(add_kernel, out_shape=jax.ShapeDtypeStruct((T, D), BF16),...]
  transfers between devices with their start and end apart: 0 -> 2, of which waited for: 0 -> 0; matrix products, arithmetic and copies ran while one was open for 0% -> 0% of each run, Pallas kernels for 0% -> 19%
where the time goes in v6:
time: 42.7 us; the launch traced here: 42.6 us
  Pallas kernels  38.6 us (90%)
  starting transfers between devices  3.32 us (8%)
  between operations  0.67 us (2%)
    pallas_call x1, Pallas kernels, per_device(): pl.pallas_call(functools.partial(moe_kernel, dims), out_shape=[vm(*r) for...  29.9 us
    pallas_call x1, Pallas kernels, per_device(): pl.pallas_call(functools.partial(write_kernel, E), out_shape=[jax.ShapeDt...  8.01 us
    ppermute x1, starting transfers between devices, per_device(): from_right = lax.ppermute(to_left, 'ep', [(b, a) for a, b in ahead])  2.05 us
    ppermute x1, starting transfers between devices, per_device(): from_left = lax.ppermute(to_right, 'ep', ahead)  1.27 us
  transfers between devices with their start and end apart: 2, of which 0 were waited for; matrix products, arithmetic and copies ran while one was open for 0% of the time, Pallas kernels for 19%

profile of v6, /device:TPU:120, one launch (start us, length us, event | category | flops | bytes accessed | tf_op | source)
XLA Modules:
  0.0 42.6 jit_solution(593694997437112977)
XLA Ops:
  0.6 29.9 %moe_exchange.1 = (bf16[5,1536,512]{2,1,0:T(8,128)(2,1)S(1)}, bf16[5,1536,512]{2,1,0:T(8,128)(2,1)S(1)}, bf16[5,128,1536]{2,1,0:T(8,128)(2,1)S(1)}, bf16[5,128,1...) custom-call(bf16[32,1536]{1,0:T(8,128)(2,1)} %x_hbm.1, ...), custom_call_target="tpu_custom_call" | custom-call | tf_op jit(solution)/shard_map/moe_exchange/pallas_call | solution.py:495
  30.5 1.3 %collective-permute-start = (f32[32,1536]{1,0:T(8,128)S(1)}, f32[32,1536]{1,0:T(8,128)S(1)}, u32[]{:S(2)}, u32[]{:S(2)}) collective-permute-start(f32[32,1536]{1,0:T(8,128)S(1)} %get-tuple-element.32), channel_id=1, source_target_pairs={{0,2},{1,3},{2,4},{3,5},{4,6},{5,7},{6,0},{7,1},{8,10},{9,11},{10,... | collective-permute-start | bytes 589832 | tf_op jit(solution)/shard_map/ppermute | solution.py:519
  31.8 2.1 %collective-permute-start.1 = (f32[32,1536]{1,0:T(8,128)S(1)}, f32[32,1536]{1,0:T(8,128)S(1)}, u32[]{:S(2)}, u32[]{:S(2)}) collective-permute-start(f32[32,1536]{1,0:T(8,128)S(1)} %get-tuple-element.33), channel_id=1, source_target_pairs={{2,0},{3,1},{4,2},{5,3},{6,4},{7,5},{0,6},{1,7},{10,8},{11,9},{12,... | collective-permute-start | bytes 589832 | tf_op jit(solution)/shard_map/ppermute | solution.py:520
  33.9 8.0 %write_results.1 = (bf16[5,1536,512]{2,1,0:T(8,128)(2,1)}, bf16[5,1536,512]{2,1,0:T(8,128)(2,1)}, bf16[5,512,1536]{2,1,0:T(8,128)(2,1)}, bf16[32,1536]{1,0:T(8,128)(2,1)}, f32[8,32]{1,0:T(8,128)}) custom-call(bf16[5,1536,512]{2,1,0:T(8,128)(2,1)S(1)} %get-tuple-element.22.g1, bf16[5,1536,512]{2,1,0:T(8,128)(2,1)S(1)} %get-tuple-element.23.g3, ...), custom_call_target="tpu_custom_call" | custom-call | flops 2013265920 | bytes 23592960 | tf_op jit(solution)/shard_map/write_results/pallas_call | solution.py:521
  41.9 0.0 collective-permute-done.from_left
  41.9 0.0 collective-permute-done.1.from_right
  41.9 0.7 %add_partials.1 = bf16[32,1536]{1,0:T(8,128)(2,1)} custom-call(f32[32,1536]{1,0:T(8,128)S(1)} %get-tuple-element.31.own, f32[32,1536]{1,0:T(8,128)S(1)} %collective-permute-done.from_left, f32[32,1536]{1,0:T(8,128)S(1)} %collective-permute-done.1.from_right), custom_call_target="tpu_custom_call" | custom-call | tf_op jit(solution)/shard_map/add_partials/pallas_call | solution.py:532
Async XLA Ops:
  30.5 11.3 %collective-permute-start = (f32[32,1536]{1,0:T(8,128)S(1)}, f32[32,1536]{1,0:T(8,128)S(1)}, u32[]{:S(2)}, u32[]{:S(2)}) collective-permute-start(f32[32,1536]{1,0:T(8,128)S(1)} %get-tuple-element.32), channel_id=1, source_target_pairs={{0,2},{1,3},{2,4},{3,5},{4,6},{5,7},{6,0},{7,1},{8,10},{9,11},{10,... | collective-permute-start | bytes 589832 | tf_op jit(solution)/shard_map/ppermute | solution.py:519
  31.8 10.1 %collective-permute-start.1 = (f32[32,1536]{1,0:T(8,128)S(1)}, f32[32,1536]{1,0:T(8,128)S(1)}, u32[]{:S(2)}, u32[]{:S(2)}) collective-permute-start(f32[32,1536]{1,0:T(8,128)S(1)} %get-tuple-element.33), channel_id=1, source_target_pairs={{2,0},{3,1},{4,2},{5,3},{6,4},{7,5},{0,6},{1,7},{10,8},{11,9},{12,... | collective-permute-start | bytes 589832 | tf_op jit(solution)/shard_map/ppermute | solution.py:520

commit v7 on v6

--- a/solution.py
+++ b/solution.py
@@ -12,8 +12,7 @@
 LANES = 128
 N_CHUNK = 3
 TB = 256
-EARLY = 2
-SLOTS = 3
+EARLY = 3
 
 
 def capacity_of(tok_dev, top_k, n_experts):
@@ -45,7 +44,7 @@
                w1, w3, r_all, dy_all, h_all, dab_all, out_ref, gg_ref, own_ref, tor_ref, tol_ref,
                w2, w1t, w2t, xg, meta, idx_v, slot_v, gate_v, scr, tok, c1_all, c2_all,
                p_all, comb, y_all, part, sibbuf, ringbuf, finbuf, ggsrc, ggbuf,
-               w_sem, loc_sem, meta_ss, meta_rs, ag_ss, ag_rs, rt_ss, rt_rs, gg_sem):
+               w_sem, loc_sem, meta_ss, meta_rs, ag_ss, ag_rs, rt_ss, rt_rs, fin_sem, gg_sem):
     G, T, D, F, E, C, K = dims
     NQ = G // 2
     RW, NT = G * C, G * T
@@ -290,7 +289,8 @@
         else:
             i = 0 if n == 7 else 1
             src, dst, tgt = part.at[t, rows(left), half(j, i)], finbuf.at[u, 1, :, c_half[i]], left
-        return remote(src, dst, rt_ss.at[t], rt_rs.at[u, (0, 0, 0, 0, 1, 2, 3, 4, 3, 4)[n]], tgt)
+        rs = fin_sem if n > 5 else rt_rs.at[u, (3, 0, 0, 0, 1, 2)[n]]
+        return remote(src, dst, rt_ss.at[t], rs, tgt)
 
     def ret_0(t, j):
         for n in range(4):
@@ -298,8 +298,11 @@
 
     def ret_1(t, j):
         u = t * N_CHUNK + j
-        wait_bytes(sibbuf.at[u], rt_rs.at[u, 0])
         for n, d in enumerate((opp, right, left, me)):
+            if n == 0:
+                wait_bytes(sibbuf.at[u, 0], rt_rs.at[u, 3])
+            if n == 1:
+                wait_bytes(sibbuf.at[u, pl.ds(1, NQ - 1)], rt_rs.at[u, 0])
             part[t, rows(d), cols(j)] += sibbuf[u, n]
             for m in ((4, 5), (6,), (7,), ())[n]:
                 if t == 0 or m < 6:
@@ -321,8 +324,6 @@
 
     def ret_3(t, j, res_ref):
         u = t * N_CHUNK + j
-        wait_bytes(finbuf.at[u, 0], rt_rs.at[u, 3])
-        wait_bytes(finbuf.at[u, 1], rt_rs.at[u, 4])
         res_ref[:, cols(j)] = (part[t, rows(me), cols(j)] + finbuf[u, 0] + finbuf[u, 1]).astype(BF16)
 
     def put_rows(e, j, val):
@@ -409,13 +410,13 @@
     ret_1(1, 1)
     ret_1(1, 2)
     up_grads(r_all, dab_all, 0, w1, w3, 0)
-    up_grads(r_all, dab_all, 1, w1, w3, 1)
+    for e in range(1, EARLY):
+        up_grads(r_all, dab_all, e, w1, w3, e)
     ret_2(1, 0)
+    wait_bytes(finbuf, fin_sem)
     for j in range(N_CHUNK):
         ret_3(0, j, out_ref)
     ret_2(1, 1)
-    for e in range(2, EARLY):
-        up_grads(r_all, dab_all, e, w1, w3, e)
     tot = ggsrc[me // per_tile]
     wait_bytes(ggbuf, gg_sem.at[1])
     for d in range(1, G):
@@ -439,27 +440,19 @@
     for e in range(EARLY):
         send(g1.at[e], g1_hbm.at[e], 0)
         send(g3.at[e], g3_hbm.at[e], 1)
-    send(out, out_hbm, 2)
-    send(gg, gg_hbm, 3)
+    send(out, out_hbm, 3)
+    send(gg, gg_hbm, 4)
+    for e in range(EARLY, n_exp):
+        n = e - EARLY
+        up_grads(r, dab, e, late1, late3, n)
+        send(late1.at[n], g1_hbm.at[e], 0)
+        send(late3.at[n], g3_hbm.at[e], 1)
     F = h.shape[2]
-
-    def down_copy(e):
-        return pltpu.make_async_copy(g2.at[e % SLOTS], g2_hbm.at[e], sem.at[4 + e % SLOTS])
-
     for e in range(n_exp):
-        if e >= SLOTS:
-            down_copy(e - SLOTS).wait()
         for m in range(0, F, TB):
-            g2[e % SLOTS, pl.ds(m, TB), :] = dot_tn(h[e, :, pl.ds(m, TB)], dy[e]).astype(BF16)
-        down_copy(e).start()
-        if e >= EARLY:
-            n = e - EARLY
-            up_grads(r, dab, e, late1, late3, n)
-            send(late1.at[n], g1_hbm.at[e], 0)
-            send(late3.at[n], g3_hbm.at[e], 1)
-    for e in range(n_exp - SLOTS, n_exp):
-        down_copy(e).wait()
-    for k, ref in enumerate((g1_hbm, g3_hbm, out_hbm, gg_hbm)):
+            g2[e, pl.ds(m, TB), :] = dot_tn(h[e, :, pl.ds(m, TB)], dy[e]).astype(BF16)
+        send(g2.at[e], g2_hbm.at[e], 2)
+    for k, ref in enumerate((g1_hbm, g3_hbm, g2_hbm, out_hbm, gg_hbm)):
         pltpu.make_async_copy(ref, ref, sem.at[k]).wait()
 
 
@@ -509,7 +502,7 @@
                 vm((n_units, 2, T, CW // 2), F32), vm((N_CHUNK, 2, T, CW), F32),
                 vm((NT // LANES, K, LANES), F32), vm((G - 1, K, LANES), F32),
                 dma((E + 1,)), dma((5,)), dma, dma((4,)),
-                dma((2,)), dma((2, 7)), dma((2,)), dma((n_units, 5)), dma((2,)),
+                dma((2,)), dma((2, 7)), dma((2,)), dma((n_units, 4)), dma, dma((2,)),
             ],
             compiler_params=pltpu.CompilerParams(
                 collective_id=0, has_side_effects=True, vmem_limit_bytes=39 * 2 ** 20),
@@ -523,8 +516,8 @@
             out_shape=[jax.ShapeDtypeStruct(*r) for r in results],
             in_specs=[vspec] * len(held),
             out_specs=[aspec] * len(results),
-            scratch_shapes=[vm((E - EARLY, D, F), BF16), vm((E - EARLY, D, F), BF16), vm((SLOTS, F, D), BF16),
-                            dma((4 + SLOTS,))],
+            scratch_shapes=[vm((E - EARLY, D, F), BF16), vm((E - EARLY, D, F), BF16), vm((E, F, D), BF16),
+                            dma((len(results),))],
             compiler_params=pltpu.CompilerParams(vmem_limit_bytes=15 * 2 ** 20),
             cost_estimate=pl.CostEstimate(flops=4 * E * RW * D * F, bytes_accessed=6 * E * D * F, transcendentals=0),
             name="write_results",

time: 42.7 us -> 42.6 us (level)
  no operation moved by 1% of the time
where the time goes in v7:
time: 42.6 us; the launch traced here: 42.5 us
  Pallas kernels  38.5 us (90%)
  starting transfers between devices  3.32 us (8%)
  between operations  0.67 us (2%)
    pallas_call x1, Pallas kernels, per_device(): pl.pallas_call(functools.partial(moe_kernel, dims), out_shape=[vm(*r) for...  29.8 us
    pallas_call x1, Pallas kernels, per_device(): pl.pallas_call(functools.partial(write_kernel, E), out_shape=[jax.ShapeDt...  7.98 us
    ppermute x1, starting transfers between devices, per_device(): from_right = lax.ppermute(to_left, 'ep', [(b, a) for a, b in ahead])  2.05 us
    ppermute x1, starting transfers between devices, per_device(): from_left = lax.ppermute(to_right, 'ep', ahead)  1.28 us
  transfers between devices with their start and end apart: 2, of which 0 were waited for; matrix products, arithmetic and copies ran while one was open for 0% of the time, Pallas kernels for 19%

profile of v7, /device:TPU:120, one launch (start us, length us, event | category | flops | bytes accessed | tf_op | source)
XLA Modules:
  0.0 42.5 jit_solution(8062498416213519446)
XLA Ops:
  0.6 29.8 %moe_exchange.1 = (bf16[5,1536,512]{2,1,0:T(8,128)(2,1)S(1)}, bf16[5,1536,512]{2,1,0:T(8,128)(2,1)S(1)}, bf16[5,128,1536]{2,1,0:T(8,128)(2,1)S(1)}, bf16[5,128,1...) custom-call(bf16[32,1536]{1,0:T(8,128)(2,1)} %x_hbm.1, ...), custom_call_target="tpu_custom_call" | custom-call | tf_op jit(solution)/shard_map/moe_exchange/pallas_call | solution.py:488
  30.5 1.3 %collective-permute-start = (f32[32,1536]{1,0:T(8,128)S(1)}, f32[32,1536]{1,0:T(8,128)S(1)}, u32[]{:S(2)}, u32[]{:S(2)}) collective-permute-start(f32[32,1536]{1,0:T(8,128)S(1)} %get-tuple-element.32), channel_id=1, source_target_pairs={{0,2},{1,3},{2,4},{3,5},{4,6},{5,7},{6,0},{7,1},{8,10},{9,11},{10,... | collective-permute-start | bytes 589832 | tf_op jit(solution)/shard_map/ppermute | solution.py:512
  31.8 2.0 %collective-permute-start.1 = (f32[32,1536]{1,0:T(8,128)S(1)}, f32[32,1536]{1,0:T(8,128)S(1)}, u32[]{:S(2)}, u32[]{:S(2)}) collective-permute-start(f32[32,1536]{1,0:T(8,128)S(1)} %get-tuple-element.33), channel_id=1, source_target_pairs={{2,0},{3,1},{4,2},{5,3},{6,4},{7,5},{0,6},{1,7},{10,8},{11,9},{12,... | collective-permute-start | bytes 589832 | tf_op jit(solution)/shard_map/ppermute | solution.py:513
  33.8 8.0 %write_results.1 = (bf16[5,1536,512]{2,1,0:T(8,128)(2,1)}, bf16[5,1536,512]{2,1,0:T(8,128)(2,1)}, bf16[5,512,1536]{2,1,0:T(8,128)(2,1)}, bf16[32,1536]{1,0:T(8,128)(2,1)}, f32[8,32]{1,0:T(8,128)}) custom-call(bf16[5,1536,512]{2,1,0:T(8,128)(2,1)S(1)} %get-tuple-element.22.g1, bf16[5,1536,512]{2,1,0:T(8,128)(2,1)S(1)} %get-tuple-element.23.g3, ...), custom_call_target="tpu_custom_call" | custom-call | flops 2013265920 | bytes 23592960 | tf_op jit(solution)/shard_map/write_results/pallas_call | solution.py:514
  41.8 0.0 collective-permute-done.from_left
  41.8 0.0 collective-permute-done.1.from_right
  41.8 0.7 %add_partials.1 = bf16[32,1536]{1,0:T(8,128)(2,1)} custom-call(f32[32,1536]{1,0:T(8,128)S(1)} %get-tuple-element.31.own, f32[32,1536]{1,0:T(8,128)S(1)} %collective-permute-done.from_left, f32[32,1536]{1,0:T(8,128)S(1)} %collective-permute-done.1.from_right), custom_call_target="tpu_custom_call" | custom-call | tf_op jit(solution)/shard_map/add_partials/pallas_call | solution.py:525
Async XLA Ops:
  30.5 11.3 %collective-permute-start = (f32[32,1536]{1,0:T(8,128)S(1)}, f32[32,1536]{1,0:T(8,128)S(1)}, u32[]{:S(2)}, u32[]{:S(2)}) collective-permute-start(f32[32,1536]{1,0:T(8,128)S(1)} %get-tuple-element.32), channel_id=1, source_target_pairs={{0,2},{1,3},{2,4},{3,5},{4,6},{5,7},{6,0},{7,1},{8,10},{9,11},{10,... | collective-permute-start | bytes 589832 | tf_op jit(solution)/shard_map/ppermute | solution.py:512
  31.8 10.0 %collective-permute-start.1 = (f32[32,1536]{1,0:T(8,128)S(1)}, f32[32,1536]{1,0:T(8,128)S(1)}, u32[]{:S(2)}, u32[]{:S(2)}) collective-permute-start(f32[32,1536]{1,0:T(8,128)S(1)} %get-tuple-element.33), channel_id=1, source_target_pairs={{2,0},{3,1},{4,2},{5,3},{6,4},{7,5},{0,6},{1,7},{10,8},{11,9},{12,... | collective-permute-start | bytes 589832 | tf_op jit(solution)/shard_map/ppermute | solution.py:513
